TPU v7x, 32 devices: a whole 2x2x4 slice. The times are simulated.
32 devices in a mesh: dp: 8 (over z, y), mp: 4 (over x, core).
Axes of the slice: x: 2, y: 2, z: 4, core: 2. Of those that a mesh axis runs over, the one named last changes fastest.
Arguments:
- pred_input: bfloat16 [512, 256, 384], P('dp'), may hold values from -6 to 6
- proj_weight: bfloat16 [384, 1280], P('dp', 'mp'), may hold values from -0.3125 to 0.3125
- proj_bias: float32 [1280], P('mp'), may hold values from -3 to 3
- targets: bfloat16 [512, 256, 1280], P('dp', None, 'mp'), may hold values from -6 to 6
- block_masks: int32 [512, 4, 256], P('dp'), may hold values from 0 to 1, as said below
Outputs:
- loss: float32 [], replicated
- clip_scale: float32 [], replicated
- grad_weight: float32 [384, 1280], P('dp', 'mp')
- grad_bias: float32 [1280], P('mp')
Inputs may be any that keep to these rules, and one draw needn't show every extreme that they name: `block_masks`: each of an image's 4 target blocks is a nonempty rectangle of patches on the 16 x 16 grid (row-major patch order); blocks may intersect.
All inputs are finite; a program needn't handle non-finite values.
Results may differ from a plain program's by a relative error of at most 0.0003.
Values may be sent and summed in bfloat16 or wider, within the bound.
A program may use at most 192 MiB of HBM per device.

v0:
```python
import functools

import jax
import jax.numpy as jnp
from jax import lax
from jax.experimental import pallas as pl
from jax.experimental.pallas import tpu as pltpu
from jax.sharding import PartitionSpec as P

F32 = jnp.float32
BF16 = jnp.bfloat16
MESH = pl.DeviceIdType.MESH
LANES = 128
GROUP = 8
PAIR = 2
CHUNK = 16


def pad_to(n, m):
    return (n + m - 1) // m * m


def layout(rows, feat):
    starts, at = [], 0
    for _ in range(feat // LANES):
        starts.append(at)
        at += pad_to(rows, 8)
    if feat % LANES:
        starts.append(at)
        at += pad_to(rows // 2, 8)
    starts.append(at)
    return starts, at + 8


def finish(ndp, nmp, sum_ref, fin_ref, loss_ref, clip_ref, gw_ref, gb_ref):
    rows, feat = gw_ref.shape
    starts, _ = layout(rows, feat)
    tiles = pad_to(feat, LANES) // LANES
    count = sum_ref[starts[-1] + tiles + 1:starts[-1] + tiles + 2, 0:1]
    square, loss = fin_ref[:, 0:1], fin_ref[:, 1:2]
    norm = jnp.sqrt(square) / count
    scale = jnp.minimum(1.0, 1.0 / (norm + 1e-06))
    factor = scale / count
    loss_ref[...] = loss / count * (1.0 / (feat * nmp * ndp))
    clip_ref[...] = scale
    for n in range(feat // LANES):
        gw_ref[:, n * LANES:(n + 1) * LANES] = sum_ref[starts[n]:starts[n] + rows, :] * factor
    half = LANES // 2
    if feat % LANES:
        packed = sum_ref[starts[-2]:starts[-2] + rows // 2, :] * factor
        gw_ref[:rows // 2, feat - half:] = packed[:, :half]
        gw_ref[rows // 2:, feat - half:] = packed[:, half:]
    for n in range(tiles):
        stop = min((n + 1) * LANES, feat)
        bias = sum_ref[starts[-1] + n:starts[-1] + n + 1, :] * factor
        gb_ref[n * LANES:stop] = bias[0, :stop - n * LANES]


def kernel(ndp, nmp, x_hbm, w_ref, b_ref, t_hbm, m_hbm,
           out_ref, fin_ref,
           xv, tv, mv, wall, wfull, wt, bcol, brow, ssend, srecv, rbuf, mbuf, cbuf,
           pa, pb, sa, sb, acc, gacc, lacc, gsend, pairv, gmid, grecv, fsend, frecv,
           xsem, tsem, msem, wss, wrs, sss, srs, pss, prs, gss, grs, fss, frs):
    images, feat, patches = tv.shape
    width = xv.shape[1]
    rows = w_ref.shape[0]
    dp, mp = lax.axis_index("dp"), lax.axis_index("mp")
    inner_dp = gsend.shape[0]
    outer_dp = gsend.shape[1]
    near, far = lax.rem(dp, inner_dp), dp // inner_dp
    featp = acc.shape[0]
    groups = images // GROUP
    ntot = ndp * nmp
    me = dp * nmp + mp
    feat_full = feat * nmp

    def t_copy(g):
        s = pl.ds(g * GROUP, GROUP)
        return pltpu.make_async_copy(t_hbm.at[s], tv.at[s], tsem.at[g])

    def x_copy(g):
        s = pl.ds(g * GROUP * patches, GROUP * patches)
        return pltpu.make_async_copy(x_hbm.at[s], xv.at[s], xsem.at[g])

    m_copy = pltpu.make_async_copy(m_hbm, mv, msem)

    barrier = pltpu.get_barrier_semaphore()

    for g in range(groups):
        t_copy(g).start()
    m_copy.start()

    def greet(o, _):
        d = lax.rem(me + o, ntot)
        pl.semaphore_signal(barrier, inc=1, device_id=(d // nmp, lax.rem(d, nmp)), device_id_type=MESH)
        return 0

    lax.fori_loop(1, ntot, greet, 0)
    acc[...] = jnp.zeros_like(acc)
    gacc[...] = jnp.zeros_like(gacc)
    lacc[...] = jnp.zeros_like(lacc)
    sb[...] = jnp.zeros_like(sb)
    wfull[...] = jnp.zeros_like(wfull)
    brow[...] = jnp.zeros_like(brow)
    brow[0:1, :feat] = b_ref[...].reshape(1, feat)
    bcol[...] = jnp.transpose(jnp.broadcast_to(brow[0:1, :], (LANES, featp)))

    pl.semaphore_wait(barrier, ntot - 1)

    def w_copy(o):
        return pltpu.make_async_remote_copy(
            src_ref=w_ref, dst_ref=wall.at[o - 1], send_sem=wss.at[o - 1], recv_sem=wrs.at[o - 1],
            device_id=(lax.rem(dp + o, ndp), mp), device_id_type=MESH)

    for o in range(1, ndp):
        w_copy(o).start()

    def s_copy(o, g):
        return pltpu.make_async_remote_copy(
            src_ref=ssend.at[g], dst_ref=srecv.at[o - 1, g],
            send_sem=sss.at[o - 1, g], recv_sem=srs.at[o - 1, g],
            device_id=(dp, lax.rem(mp + o, nmp)), device_id_type=MESH)

    m_copy.wait()

    def cover(g, _):
        block = [jnp.sum(mv[g * GROUP + j], axis=0, keepdims=True) for j in range(GROUP)]
        cbuf[pl.ds(pl.multiple_of(g * GROUP, GROUP), GROUP), :] = jnp.concatenate(block, axis=0).astype(F32)
        return 0

    lax.fori_loop(0, groups, cover, 0)

    def stats(g, _):
        t_copy(g).wait()

        @pl.when(g >= 2)
        def _():
            x_copy(g - 2).start()

        sums, squares = [], []
        for j in range(GROUP):
            i = g * GROUP + j
            part = jnp.zeros((CHUNK, patches), F32)
            for c in range(0, feat, CHUNK):
                part = part + tv[i, c:c + CHUNK, :].astype(F32)
            total = jnp.sum(part, axis=0, keepdims=True)
            mean = total * (1.0 / feat)
            part = jnp.zeros((CHUNK, patches), F32)
            for c in range(0, feat, CHUNK):
                centred = tv[i, c:c + CHUNK, :].astype(F32) - mean
                part = part + centred * centred
            sums.append(total)
            squares.append(jnp.sum(part, axis=0, keepdims=True))
        ssend[g] = jnp.concatenate(sums + squares, axis=0)

        @pl.when(g > 0)
        def _():
            for o in range(1, nmp):
                s_copy(o, g - 1).start()

        return 0

    lax.fori_loop(0, groups, stats, 0)
    for g in range(groups - 2, groups):
        x_copy(g).start()

    def place(owner_static, block):
        wfull[owner_static * rows:(owner_static + 1) * rows, :feat] = block.astype(F32)

    for o in range(1, ndp):
        w_copy(o).wait_recv()
    for o in range(1, nmp):
        s_copy(o, groups - 1).start()
    for k in range(ndp):
        slot = lax.rem(dp - k + ndp, ndp)
        other = wall[jnp.maximum(slot - 1, 0)].astype(F32)
        mine = w_ref[...].astype(F32)
        place(k, jnp.where(slot == 0, mine, other))
    wt[...] = jnp.transpose(wfull[...])[:feat].astype(BF16)

    def x_rows(k):
        n = PAIR * patches
        return xv[pl.ds(pl.multiple_of(k * n, n), n), :]

    def project(p_ref, k):
        p_ref[...] = lax.dot_general(wt[...], x_rows(k), (((1,), (1,)), ((), ())), preferred_element_type=F32)

    def gradient(s_ref, k):
        acc[:feat, :] += jnp.dot(s_ref[...], x_rows(k), preferred_element_type=F32)

    def pointwise(p_ref, s_ref, k):
        img = k * PAIR
        rs = [rbuf[pl.ds(img + g, 1), :] for g in range(PAIR)]
        ms = [mbuf[pl.ds(img + g, 1), :] for g in range(PAIR)]
        cs = [cbuf[pl.ds(img + g, 1), :] for g in range(PAIR)]
        loss = jnp.zeros((CHUNK, patches), F32)
        for c in range(0, feat, CHUNK):
            bias = bcol[c:c + CHUNK, :]
            bias = jnp.concatenate([bias] * (patches // LANES), axis=1)
            total = jnp.zeros((CHUNK, LANES), F32)
            for g in range(PAIR):
                cols = slice(g * patches, (g + 1) * patches)
                t = tv[img + g, c:c + CHUNK, :].astype(F32)
                differ = (p_ref[c:c + CHUNK, cols] + bias) + (ms[g] - t * rs[g])
                clipped = jnp.clip(differ, -1.0, 1.0)
                source = clipped * cs[g]
                loss = loss + source * (differ - 0.5 * clipped)
                for h in range(0, patches, LANES):
                    total = total + source[:, h:h + LANES]
                s_ref[c:c + CHUNK, cols] = source.astype(BF16)
            gacc[c:c + CHUNK, :] += total
        lacc[...] += loss

    x_copy(0).wait()
    project(pa, 0)
    steps = images // PAIR
    per_group = GROUP // PAIR

    def outer(g, _):
        @pl.when(g + 1 < groups)
        def _():
            x_copy(g + 1).wait()

        for o in range(1, nmp):
            s_copy(o, g).wait_recv()
        parts = [ssend[g]] + [srecv[o - 1, g] for o in range(1, nmp)]
        sums = [p[:GROUP] for p in parts]
        mean = functools.reduce(jnp.add, sums) * (1.0 / feat_full)
        var = functools.reduce(jnp.add, [p[GROUP:] for p in parts])
        for s in sums:
            gap = s * (1.0 / feat) - mean
            var = var + feat * (gap * gap)
        rstd = lax.rsqrt(var * (1.0 / feat_full) + 1e-05)
        here = pl.ds(pl.multiple_of(g * GROUP, GROUP), GROUP)
        rbuf[here, :] = rstd
        mbuf[here, :] = mean * rstd

        def inner(j, _):
            k = g * per_group + 2 * j
            pointwise(pa, sa, k)
            project(pb, k + 1)
            gradient(sb, jnp.maximum(k - 1, 0))
            pointwise(pb, sb, k + 1)
            project(pa, jnp.minimum(k + 2, steps - 1))
            gradient(sa, k)
            return 0

        lax.fori_loop(0, per_group // 2, inner, 0)
        return 0

    lax.fori_loop(0, groups, outer, 0)
    gradient(sb, steps - 1)

    bias_part = jnp.sum(jnp.transpose(gacc[...]), axis=0, keepdims=True)
    loss_part = jnp.sum(lacc[...], keepdims=True)
    count_part = jnp.sum(cbuf[...], keepdims=True)
    at_row = lax.broadcasted_iota(jnp.int32, (8, LANES), 0)
    tiles = featp // LANES
    extra = jnp.where(at_row == tiles, loss_part, count_part)
    for n in range(tiles):
        extra = jnp.where(at_row == n, bias_part[:, n * LANES:(n + 1) * LANES], extra)
    starts, total_rows = layout(rows, feat)
    full = jnp.transpose(acc[...])
    for k in range(ndp):
        slot = gsend.at[k % inner_dp, k // inner_dp]
        if rows % 16:
            slot[...] = jnp.zeros(slot.shape, F32)
        mine = full[k * rows:(k + 1) * rows]
        for n in range(feat // LANES):
            slot[starts[n]:starts[n] + rows, :] = mine[:, n * LANES:(n + 1) * LANES]
        if feat % LANES:
            slot[starts[-2]:starts[-2] + rows // 2, :] = jnp.concatenate(
                [mine[:rows // 2, feat - LANES // 2:feat], mine[rows // 2:, feat - LANES // 2:feat]], axis=1)
        slot[starts[-1]:, :] = extra

    other = 1 - near

    def p_copy(o):
        to = lax.rem(far + o, outer_dp)
        return pltpu.make_async_remote_copy(
            src_ref=gsend.at[other, to], dst_ref=pairv.at[o], send_sem=pss.at[o], recv_sem=prs.at[o],
            device_id=(far * inner_dp + other, mp), device_id_type=MESH)

    def g_copy(o):
        to = lax.rem(far + o, outer_dp)
        return pltpu.make_async_remote_copy(
            src_ref=gmid.at[o - 1], dst_ref=grecv.at[o - 1], send_sem=gss.at[o - 1], recv_sem=grs.at[o - 1],
            device_id=(to * inner_dp + near, mp), device_id_type=MESH)

    order = list(range(1, outer_dp)) + [0]
    for o in order:
        p_copy(o).start()
    for o in order:
        p_copy(o).wait_recv()
        pair = gsend[near, lax.rem(far + o, outer_dp)] + pairv[o]
        if o:
            gmid[o - 1] = pair
            g_copy(o).start()
    for o in range(1, outer_dp):
        g_copy(o).wait_recv()
        pair = pair + grecv[o - 1]
    out_ref[...] = pair
    grad = pair[:starts[-1]]
    sums = pair[starts[-1]:]
    bias_grad = sums[:tiles]
    square = jnp.sum(grad * grad, keepdims=True)
    bias_square = jnp.sum(bias_grad * bias_grad, keepdims=True)
    lane = lax.broadcasted_iota(jnp.int32, (1, LANES), 1)
    fsend[...] = jnp.where(lane == 0, square + bias_square * (1.0 / ndp), sums[tiles:tiles + 1, :])

    def f_copy(o):
        d = lax.rem(me + o, ntot)
        return pltpu.make_async_remote_copy(
            src_ref=fsend, dst_ref=frecv.at[o - 1], send_sem=fss.at[o - 1], recv_sem=frs.at[o - 1],
            device_id=(d // nmp, lax.rem(d, nmp)), device_id_type=MESH)

    def f_start(o, _):
        f_copy(o).start()
        return 0

    def f_wait(o, _):
        f_copy(o).wait_recv()
        return 0

    lax.fori_loop(1, ntot, f_start, 0)
    lax.fori_loop(1, ntot, f_wait, 0)
    fin_ref[...] = fsend[...] + jnp.sum(frecv[...], axis=0)

    for o in range(1, ndp):
        w_copy(o).wait_send()
    for o in order:
        p_copy(o).wait_send()
        if o:
            g_copy(o).wait_send()

    def s_drain(g, _):
        for o in range(1, nmp):
            s_copy(o, g).wait_send()
        return 0

    def f_drain(o, _):
        f_copy(o).wait_send()
        return 0

    lax.fori_loop(0, groups, s_drain, 0)
    lax.fori_loop(1, ntot, f_drain, 0)


def body(pred_input, proj_weight, proj_bias, targets, block_masks):
    images, patches, width = pred_input.shape
    feat = targets.shape[2]
    rows = proj_weight.shape[0]
    blocks = block_masks.shape[1]
    ndp, nmp = lax.axis_size("dp"), lax.axis_size("mp")
    ntot = ndp * nmp
    featp = pad_to(feat, LANES)
    groups = images // GROUP
    dma = pltpu.SemaphoreType.DMA
    vmem = pl.BlockSpec(memory_space=pltpu.VMEM)
    hbm = pl.BlockSpec(memory_space=pl.ANY)
    _, total_rows = layout(rows, feat)
    inner_dp = 2
    outer_dp = ndp // inner_dp
    summed, final = pl.pallas_call(
        functools.partial(kernel, ndp, nmp),
        out_shape=(
            jax.ShapeDtypeStruct((total_rows, LANES), F32),
            jax.ShapeDtypeStruct((1, LANES), F32),
        ),
        in_specs=[hbm, vmem, vmem, hbm, hbm],
        out_specs=(vmem,) * 2,
        scratch_shapes=[
            pltpu.VMEM((images * patches, width), BF16),
            pltpu.VMEM((images, feat, patches), BF16),
            pltpu.VMEM((images, blocks, patches), jnp.int32),
            pltpu.VMEM((ndp - 1, rows, feat), BF16),
            pltpu.VMEM((width, featp), F32),
            pltpu.VMEM((feat, width), BF16),
            pltpu.VMEM((featp, LANES), F32),
            pltpu.VMEM((8, featp), F32),
            pltpu.VMEM((groups, 2 * GROUP, patches), F32),
            pltpu.VMEM((nmp - 1, groups, 2 * GROUP, patches), F32),
            pltpu.VMEM((images, patches), F32),
            pltpu.VMEM((images, patches), F32),
            pltpu.VMEM((images, patches), F32),
            pltpu.VMEM((feat, PAIR * patches), F32),
            pltpu.VMEM((feat, PAIR * patches), F32),
            pltpu.VMEM((feat, PAIR * patches), BF16),
            pltpu.VMEM((feat, PAIR * patches), BF16),
            pltpu.VMEM((featp, width), F32),
            pltpu.VMEM((featp, LANES), F32),
            pltpu.VMEM((CHUNK, patches), F32),
            pltpu.VMEM((inner_dp, outer_dp, total_rows, LANES), F32),
            pltpu.VMEM((outer_dp, total_rows, LANES), F32),
            pltpu.VMEM((outer_dp - 1, total_rows, LANES), F32),
            pltpu.VMEM((outer_dp - 1, total_rows, LANES), F32),
            pltpu.VMEM((1, LANES), F32),
            pltpu.VMEM((ntot - 1, 1, LANES), F32),
            dma((groups,)), dma((groups,)), dma(()),
            dma((ndp - 1,)), dma((ndp - 1,)),
            dma((nmp - 1, groups)), dma((nmp - 1, groups)),
            dma((outer_dp,)), dma((outer_dp,)),
            dma((outer_dp - 1,)), dma((outer_dp - 1,)),
            dma((ntot - 1,)), dma((ntot - 1,)),
        ],
        compiler_params=pltpu.CompilerParams(
            collective_id=0, has_side_effects=True, vmem_limit_bytes=60 * 1024 * 1024
        ),
    )(
        pred_input.reshape(images * patches, width),
        proj_weight,
        proj_bias,
        jnp.swapaxes(targets, 1, 2),
        block_masks,
    )
    loss, clip, gw, gb = pl.pallas_call(
        functools.partial(finish, ndp, nmp),
        out_shape=(
            jax.ShapeDtypeStruct((1, 1), F32),
            jax.ShapeDtypeStruct((1, 1), F32),
            jax.ShapeDtypeStruct((rows, feat), F32),
            jax.ShapeDtypeStruct((feat,), F32),
        ),
        in_specs=[vmem] * 2,
        out_specs=(vmem,) * 4,
    )(summed, final)
    return loss.reshape(()), clip.reshape(()), gw, gb


def solution(mesh):
    in_specs = (
        P("dp", None, None),
        P("dp", "mp"),
        P("mp"),
        P("dp", None, "mp"),
        P("dp", None, None),
    )
    out_specs = (P(), P(), P("dp", "mp"), P("mp"))
    return jax.shard_map(body, mesh=mesh, in_specs=in_specs, out_specs=out_specs, check_vma=False)
```

profile of v0, /device:TPU:0, one launch (start us, length us, event | category | flops | bytes accessed | tf_op | source)
XLA Modules:
  0.0 53.7 jit_solution(10588443647334156837)
XLA Ops:
  0.6 51.4 %shard_map.84 = (f32[128,128]{1,0:T(8,128)}, f32[1,128]{1,0:T(1,128)}) custom-call(bf16[16384,384]{1,0:T(8,128)(2,1)} %bitcast.4, bf16[48,320]{1,0:T(8,128)(2,1)} %w_ref.1, f32[320]{0:T(512)} %b_ref.1, bf16[64,320,256]{2,1,0:T(8,128)(2,1)} %bitcast.5, s32[64,4,256]{2,1,0:T(4,128)} %m_hbm.1), custom_call_target="tpu_custom_call" | custom-call | tf_op jit(solution)/shard_map/pallas_call | solution.py:364
  52.0 1.6 %shard_map.85 = (f32[1,1]{1,0:T(1,128)}, f32[1,1]{1,0:T(1,128)}, f32[48,320]{1,0:T(8,128)}, f32[320]{0:T(512)}) custom-call(f32[128,128]{1,0:T(8,128)} %get-tuple-element.10.sum_ref, f32[1,128]{1,0:T(1,128)} %get-tuple-element.11.fin_ref), custom_call_target="tpu_custom_call" | custom-call | tf_op jit(solution)/shard_map/pallas_call | solution.py:416
where the time goes:
time: 53.9 us; the launch traced here: 53.7 us
  Pallas kernels  53 us (98%)
  between operations  0.64 us (1%)
    pallas_call x1, Pallas kernels, body(): pl.pallas_call(functools.partial(kernel, ndp, nmp), out_shape=(jax.ShapeD...  51.4 us
    pallas_call x1, Pallas kernels, body(): pl.pallas_call(functools.partial(finish, ndp, nmp), out_shape=(jax.ShapeD...  1.64 us

commit v1 on v0

v1 whole, which is shorter than its diff:
```python
import functools

import jax
import jax.numpy as jnp
from jax import lax
from jax.experimental import pallas as pl
from jax.experimental.pallas import tpu as pltpu
from jax.sharding import PartitionSpec as P

F32 = jnp.float32
BF16 = jnp.bfloat16
MESH = pl.DeviceIdType.MESH
LANES = 128
GROUP = 8
PAIR = 2
CHUNK = 16
TILE = 256
ROWS = 32
SWEEP = 16


def pad_to(n, m):
    return (n + m - 1) // m * m


def layout(rows):
    half = pad_to(rows, 8)
    sums = half + pad_to(rows // 2, 8)
    late = sums + 8
    return half, sums, late, late + pad_to(rows, 8)


def finish(ndp, nmp, sum_ref, fin_ref, loss_ref, clip_ref, gw_ref, gb_ref):
    rows, feat = gw_ref.shape
    half_at, sums_at, late_at, _ = layout(rows)
    tiles = pad_to(feat, LANES) // LANES
    count = sum_ref[sums_at + tiles + 1:sums_at + tiles + 2, 0:1]
    square, loss = fin_ref[:, 0:1], fin_ref[:, 1:2]
    norm = jnp.sqrt(square) / count
    scale = jnp.minimum(1.0, 1.0 / (norm + 1e-06))
    factor = scale / count
    loss_ref[...] = loss / count * (1.0 / (feat * nmp * ndp))
    clip_ref[...] = scale
    gw_ref[:, :LANES] = sum_ref[late_at:late_at + rows, :] * factor
    gw_ref[:, LANES:2 * LANES] = sum_ref[:rows, :] * factor
    half = LANES // 2
    packed = sum_ref[half_at:half_at + rows // 2, :] * factor
    gw_ref[:rows // 2, 2 * LANES:] = packed[:, :half]
    gw_ref[rows // 2:, 2 * LANES:] = packed[:, half:]
    for n in range(tiles):
        stop = min((n + 1) * LANES, feat)
        bias = sum_ref[sums_at + n:sums_at + n + 1, :] * factor
        gb_ref[n * LANES:stop] = bias[0, :stop - n * LANES]


def kernel(ndp, nmp, x_hbm, w_ref, b_ref, t_hbm, m_hbm,
           out_ref, fin_ref,
           xv, tv, mv, wall, wfull, wt, ones, bcol, brow, ssend, srecv, rbuf, mbuf, cbuf,
           pa, pb, sa, sb, s2, acc1, acc2, gacc, lacc,
           gs1, pv1, gm1, gr1, gs2, pv2, gm2, gr2, fsend, frecv,
           xsem, tsem, msem, wss, wrs, sss, srs, ps1, pr1, g1s, g1r, ps2, pr2, g2s, g2r, fss, frs):
    images, halves, feat, _ = tv.shape
    patches = halves * LANES
    parts, _, _ = xv.shape
    width = parts * LANES
    rows = w_ref.shape[0]
    early = s2.shape[2]
    rest = feat - early
    pieces = feat // ROWS
    dp, mp = lax.axis_index("dp"), lax.axis_index("mp")
    inner_dp, outer_dp = gs1.shape[0], gs1.shape[1]
    near, far = lax.rem(dp, inner_dp), dp // inner_dp
    featp = bcol.shape[0]
    groups = images // GROUP
    steps = images // PAIR
    ntot = ndp * nmp
    me = dp * nmp + mp
    feat_full = feat * nmp
    mxus = range(2)

    def scoped(*accs):
        proj = [list(accs[q * pieces:(q + 1) * pieces]) for q in mxus]
        grad_acc = list(accs[2 * pieces:2 * pieces + 2])
        late_acc = list(accs[2 * pieces + 2:2 * pieces + 4])

        def t_copy(g, h):
            s = pl.ds(g * GROUP, GROUP)
            return pltpu.make_async_copy(t_hbm.at[s, :, pl.ds(h * LANES, LANES)], tv.at[s, h], tsem.at[h, g])

        def x_copy(g, j):
            s = pl.ds(g * GROUP * patches, GROUP * patches)
            return pltpu.make_async_copy(x_hbm.at[s, pl.ds(j * LANES, LANES)], xv.at[j, s], xsem.at[j, g])

        def x_start(g):
            for j in range(parts):
                x_copy(g, j).start()

        def x_wait(g):
            for j in range(parts):
                x_copy(g, j).wait()

        m_copy = pltpu.make_async_copy(m_hbm, mv, msem)
        barrier = pltpu.get_barrier_semaphore()

        def greet(o, _):
            d = lax.rem(me + o, ntot)
            pl.semaphore_signal(barrier, inc=1, device_id=(d // nmp, lax.rem(d, nmp)), device_id_type=MESH)
            return 0

        lax.fori_loop(1, ntot, greet, 0)
        m_copy.start()
        for g in range(groups):
            for h in range(halves):
                t_copy(g, h).start()

        gacc[...] = jnp.zeros_like(gacc)
        lacc[...] = jnp.zeros_like(lacc)
        sb[...] = jnp.zeros_like(sb)
        acc1[...] = jnp.zeros_like(acc1)
        wfull[...] = jnp.zeros_like(wfull)
        brow[...] = jnp.zeros_like(brow)
        if rows % 16:
            gs1[...] = jnp.zeros_like(gs1)
            gs2[...] = jnp.zeros_like(gs2)
        lane = lax.broadcasted_iota(jnp.int32, ones.shape, 1)
        ones[...] = jnp.where(lane < 3, 1.0, 0.0).astype(BF16)
        brow[0:1, :feat] = b_ref[...].reshape(1, feat)
        bcol[...] = jnp.transpose(jnp.broadcast_to(brow[0:1, :], (LANES, featp)))
        bias = bcol[:feat, :]
        high = bias.astype(BF16)
        left = bias - high.astype(F32)
        mid = left.astype(BF16)
        low = (left - mid.astype(F32)).astype(BF16)
        lane = lax.broadcasted_iota(jnp.int32, (feat, LANES), 1)
        pick = jnp.where(lane == 0, high.astype(F32), jnp.where(lane == 1, mid.astype(F32), low.astype(F32)))
        wt[:, width:] = jnp.where(lane < 3, pick, 0.0).astype(BF16)
        for q in mxus:
            blank = jnp.zeros((ROWS, TILE), BF16)
            pltpu.matmul_acc_lhs(proj[q][0], blank, load_staged_rhs=0)
            pltpu.matmul_acc_lhs(proj[q][0], blank, load_staged_rhs=1)
            for ref in proj[q] + [grad_acc[q], late_acc[q]]:
                pltpu.matmul_pop(ref)

        pl.semaphore_wait(barrier, ntot - 1)

        def w_copy(o):
            return pltpu.make_async_remote_copy(
                src_ref=w_ref, dst_ref=wall.at[o - 1], send_sem=wss.at[o - 1], recv_sem=wrs.at[o - 1],
                device_id=(lax.rem(dp + o, ndp), mp), device_id_type=MESH)

        for o in range(1, ndp):
            w_copy(o).start()

        def s_copy(o, g):
            return pltpu.make_async_remote_copy(
                src_ref=ssend.at[g], dst_ref=srecv.at[o - 1, g],
                send_sem=sss.at[o - 1, g], recv_sem=srs.at[o - 1, g],
                device_id=(dp, lax.rem(mp + o, nmp)), device_id_type=MESH)

        m_copy.wait()

        def cover(g, _):
            block = [jnp.sum(mv[g * GROUP + j], axis=0, keepdims=True) for j in range(GROUP)]
            cbuf[pl.ds(pl.multiple_of(g * GROUP, GROUP), GROUP), :] = jnp.concatenate(block, axis=0).astype(F32)
            return 0

        lax.fori_loop(0, groups, cover, 0)

        def stats(g, _):
            for h in range(halves):
                t_copy(g, h).wait()

            @pl.when(g >= 2)
            def _():
                x_start(g - 2)

            sums, squares = [], []
            for j in range(GROUP):
                i = g * GROUP + j
                for h in range(halves):
                    part = jnp.zeros((CHUNK, LANES), F32)
                    for c in range(0, feat, CHUNK):
                        part = part + tv[i, h, c:c + CHUNK, :].astype(F32)
                    total = jnp.sum(part, axis=0, keepdims=True)
                    mean = total * (1.0 / feat)
                    part = jnp.zeros((CHUNK, LANES), F32)
                    for c in range(0, feat, CHUNK):
                        centred = tv[i, h, c:c + CHUNK, :].astype(F32) - mean
                        part = part + centred * centred
                    sums.append(total)
                    squares.append(jnp.sum(part, axis=0, keepdims=True))
            for h in range(halves):
                block = jnp.concatenate(sums[h::halves] + squares[h::halves], axis=0)
                ssend[g, :, h * LANES:(h + 1) * LANES] = block

            @pl.when(g > 0)
            def _():
                for o in range(1, nmp):
                    s_copy(o, g - 1).start()

            return 0

        lax.fori_loop(0, groups, stats, 0)
        for g in range(groups - 2, groups):
            x_start(g)

        for o in range(1, ndp):
            w_copy(o).wait_recv()
        for o in range(1, nmp):
            s_copy(o, groups - 1).start()
        for k in range(ndp):
            slot = lax.rem(dp - k + ndp, ndp)
            other = wall[jnp.maximum(slot - 1, 0)].astype(F32)
            block = jnp.where(slot == 0, w_ref[...].astype(F32), other)
            wfull[k * rows:(k + 1) * rows, :feat] = block
        wt[:, :width] = jnp.transpose(wfull[...])[:feat].astype(BF16)

        def x_tile(img, part):
            at = pl.ds(pl.multiple_of(img * patches, patches), patches)
            left = xv[2 * part, at, :]
            right = xv[2 * part + 1, at, :] if 2 * part + 1 < parts else ones[...]
            return jnp.concatenate([left, right], axis=1)

        def push_project(k, part):
            for q in mxus:
                tile = x_tile(PAIR * k + q, part)
                pltpu.matmul_push_rhs(tile, staging_register=part, mxu_index=q, transpose=True)

        def project(part, c):
            lhs = wt[c * ROWS:(c + 1) * ROWS, part * TILE:(part + 1) * TILE]
            for q in mxus:
                pltpu.matmul_acc_lhs(proj[q][c], lhs, load_staged_rhs=part if c == 0 else None)

        def push_gradient(k, g):
            for q in mxus:
                pltpu.matmul_push_rhs(x_tile(PAIR * k + g, q), staging_register=g, mxu_index=q)

        def gradient(s_ref, g):
            lhs = s_ref[:, g * patches:(g + 1) * patches]
            for q in mxus:
                pltpu.matmul_acc_lhs(grad_acc[q], lhs, load_staged_rhs=g)

        def keep(p_ref, c):
            for q in mxus:
                p_ref[q, c * ROWS:(c + 1) * ROWS, :] = pltpu.matmul_pop(proj[q][c])

        def pointwise(p_ref, s_ref, k, c, stat, loss):
            for f in range(c * ROWS, (c + 1) * ROWS, CHUNK):
                total = jnp.zeros((CHUNK, LANES), F32)
                for g in range(PAIR):
                    for h in range(halves):
                        lanes = slice(h * LANES, (h + 1) * LANES)
                        r, m, cov = [v[:, lanes] for v in stat[g]]
                        t = tv[PAIR * k + g, h, f:f + CHUNK, :].astype(F32)
                        differ = p_ref[g, f:f + CHUNK, lanes] + (m - t * r)
                        clipped = jnp.clip(differ, -1.0, 1.0)
                        source = clipped * cov
                        loss[h] = loss[h] + source * (differ - 0.5 * clipped)
                        total = total + source
                        if f < early:
                            s2[PAIR * k + g, h, f:f + CHUNK, :] = source.astype(BF16)
                        else:
                            at = g * patches + h * LANES
                            s_ref[f - early:f - early + CHUNK, at:at + LANES] = source.astype(BF16)
                gacc[f:f + CHUNK, :] += total

        def step(k, p_in, p_out, s_out, s_in):
            last = steps - 1
            back, ahead, beyond = jnp.maximum(k - 1, 0), jnp.minimum(k + 1, last), jnp.minimum(k + 2, last)
            stat = [[v[pl.ds(PAIR * k + g, 1), :] for v in (rbuf, mbuf, cbuf)] for g in range(PAIR)]
            loss = [jnp.zeros((CHUNK, LANES), F32)] * halves
            todo = [functools.partial(project, 0, c) for c in range(pieces)]
            todo.append(functools.partial(push_project, ahead, 1))
            todo += [functools.partial(project, 1, c) for c in range(pieces)]
            todo.append(functools.partial(push_gradient, back, 0))
            todo.append(functools.partial(gradient, s_in, 0))
            todo.append(functools.partial(push_gradient, back, 1))
            todo.append(functools.partial(push_project, beyond, 0))
            todo.append(functools.partial(gradient, s_in, 1))
            done = 0
            for c in range(pieces):
                upto = min(len(todo), pl.cdiv(len(todo) * (c + 1), pieces))
                for op in todo[done:upto]:
                    op()
                done = upto
                pointwise(p_in, s_out, k, c, stat, loss)
            for c in range(pieces):
                keep(p_out, c)
            lacc[...] += functools.reduce(jnp.add, loss)

        x_wait(0)
        push_project(0, 0)
        for c in range(pieces):
            project(0, c)
        push_project(0, 1)
        for c in range(pieces):
            project(1, c)
        push_project(1, 0)
        for c in range(pieces):
            keep(pa, c)
        per_group = GROUP // PAIR

        def outer(g, _):
            @pl.when(g + 1 < groups)
            def _():
                x_wait(g + 1)

            for o in range(1, nmp):
                s_copy(o, g).wait_recv()
            parts_in = [ssend[g]] + [srecv[o - 1, g] for o in range(1, nmp)]
            sums = [p[:GROUP] for p in parts_in]
            mean = functools.reduce(jnp.add, sums) * (1.0 / feat_full)
            var = functools.reduce(jnp.add, [p[GROUP:] for p in parts_in])
            for s in sums:
                gap = s * (1.0 / feat) - mean
                var = var + feat * (gap * gap)
            rstd = lax.rsqrt(var * (1.0 / feat_full) + 1e-05)
            here = pl.ds(pl.multiple_of(g * GROUP, GROUP), GROUP)
            rbuf[here, :] = rstd
            mbuf[here, :] = mean * rstd

            def inner(j, _):
                k = g * per_group + 2 * j
                step(k, pa, pb, sa, sb)
                pl.delay(1)
                step(k + 1, pb, pa, sb, sa)
                return 0

            lax.fori_loop(0, per_group // 2, inner, 0)
            return 0

        lax.fori_loop(0, groups, outer, 0)
        project(0, 0)
        for q in mxus:
            pltpu.matmul_pop(proj[q][0])
        for g in range(PAIR):
            push_gradient(steps - 1, g)
            gradient(sb, g)
        acc1[:rest, :TILE] = pltpu.matmul_pop(grad_acc[0])
        acc1[:rest, TILE:] = pltpu.matmul_pop(grad_acc[1])[:, :width - TILE]

        half_at, sums_at, late_at, total_rows = layout(rows)
        tiles = featp // LANES
        bias_part = jnp.sum(jnp.transpose(gacc[...]), axis=0, keepdims=True)
        loss_part = jnp.sum(lacc[...], keepdims=True)
        count_part = jnp.sum(cbuf[...], keepdims=True)
        at_row = lax.broadcasted_iota(jnp.int32, (8, LANES), 0)
        extra = jnp.where(at_row == tiles, loss_part, count_part)
        for n in range(tiles):
            extra = jnp.where(at_row == n, bias_part[:, n * LANES:(n + 1) * LANES], extra)
        full = jnp.transpose(acc1[...])
        half = LANES // 2
        for k in range(ndp):
            slot = gs1.at[k % inner_dp, k // inner_dp]
            mine = full[k * rows:(k + 1) * rows]
            slot[:rows, :] = mine[:, :LANES]
            slot[half_at:half_at + rows // 2, :] = jnp.concatenate(
                [mine[:rows // 2, LANES:LANES + half], mine[rows // 2:, LANES:LANES + half]], axis=1)
            slot[sums_at:, :] = extra

        other = 1 - near

        def p_copy(o, bufs):
            src, dst, _, _, ss, rs, _, _ = bufs
            to = lax.rem(far + o, outer_dp)
            return pltpu.make_async_remote_copy(
                src_ref=src.at[other, to], dst_ref=dst.at[o], send_sem=ss.at[o], recv_sem=rs.at[o],
                device_id=(far * inner_dp + other, mp), device_id_type=MESH)

        def g_copy(o, bufs):
            _, _, src, dst, _, _, ss, rs = bufs
            to = lax.rem(far + o, outer_dp)
            return pltpu.make_async_remote_copy(
                src_ref=src.at[o - 1], dst_ref=dst.at[o - 1], send_sem=ss.at[o - 1], recv_sem=rs.at[o - 1],
                device_id=(to * inner_dp + near, mp), device_id_type=MESH)

        first = (gs1, pv1, gm1, gr1, ps1, pr1, g1s, g1r)
        second = (gs2, pv2, gm2, gr2, ps2, pr2, g2s, g2r)
        order = list(range(1, outer_dp)) + [0]
        for o in order:
            p_copy(o, first).start()

        def push_late(img, r):
            for q in mxus:
                pltpu.matmul_push_rhs(x_tile(img, q), staging_register=r, mxu_index=q)

        push_late(0, 0)

        def sweep(k, _):
            for g in range(SWEEP):
                img = k * SWEEP + g
                push_late(jnp.minimum(img + 1, images - 1), (g + 1) % 2)
                lhs = jnp.concatenate([s2[img, h, :, :] for h in range(halves)], axis=1)
                for q in mxus:
                    pltpu.matmul_acc_lhs(late_acc[q], lhs, load_staged_rhs=g % 2)
            return 0

        lax.fori_loop(0, images // SWEEP, sweep, 0)
        acc2[:, :TILE] = pltpu.matmul_pop(late_acc[0])
        acc2[:, TILE:] = pltpu.matmul_pop(late_acc[1])[:, :width - TILE]
        for q in mxus:
            pltpu.matmul_acc_lhs(late_acc[q], jnp.zeros((early, TILE), BF16), load_staged_rhs=0)
            pltpu.matmul_pop(late_acc[q])
        full = jnp.transpose(acc2[...])
        for k in range(ndp):
            gs2[k % inner_dp, k // inner_dp, :rows, :] = full[k * rows:(k + 1) * rows]
        for o in order:
            p_copy(o, second).start()

        pairs = []
        for bufs in (first, second):
            src, dst, mid_buf = bufs[:3]
            for o in order:
                p_copy(o, bufs).wait_recv()
                pair = src[near, lax.rem(far + o, outer_dp)] + dst[o]
                if o:
                    mid_buf[o - 1] = pair
                    g_copy(o, bufs).start()
            pairs.append(pair)
        for n, bufs in enumerate((first, second)):
            for o in range(1, outer_dp):
                g_copy(o, bufs).wait_recv()
                pairs[n] = pairs[n] + bufs[3][o - 1]
        out_ref[:late_at, :] = pairs[0]
        out_ref[late_at:, :] = pairs[1]
        head = pairs[0][:sums_at]
        sums = pairs[0][sums_at:]
        bias_grad = sums[:tiles]
        square = jnp.sum(head * head, keepdims=True) + jnp.sum(pairs[1] * pairs[1], keepdims=True)
        bias_square = jnp.sum(bias_grad * bias_grad, keepdims=True)
        lane = lax.broadcasted_iota(jnp.int32, (1, LANES), 1)
        fsend[...] = jnp.where(lane == 0, square + bias_square * (1.0 / ndp), sums[tiles:tiles + 1, :])

        def f_copy(o):
            d = lax.rem(me + o, ntot)
            return pltpu.make_async_remote_copy(
                src_ref=fsend, dst_ref=frecv.at[o - 1], send_sem=fss.at[o - 1], recv_sem=frs.at[o - 1],
                device_id=(d // nmp, lax.rem(d, nmp)), device_id_type=MESH)

        def f_start(o, _):
            f_copy(o).start()
            return 0

        def f_wait(o, _):
            f_copy(o).wait_recv()
            return 0

        lax.fori_loop(1, ntot, f_start, 0)

        for o in range(1, ndp):
            w_copy(o).wait_send()
        for bufs in (first, second):
            for o in order:
                p_copy(o, bufs).wait_send()
                if o:
                    g_copy(o, bufs).wait_send()

        def s_drain(g, _):
            for o in range(1, nmp):
                s_copy(o, g).wait_send()
            return 0

        def f_drain(o, _):
            f_copy(o).wait_send()
            return 0

        lax.fori_loop(0, groups, s_drain, 0)
        lax.fori_loop(1, ntot, f_wait, 0)
        fin_ref[...] = fsend[...] + jnp.sum(frecv[...], axis=0)
        lax.fori_loop(1, ntot, f_drain, 0)

    tile = [pltpu.ACC(q)((ROWS, TILE), F32) for q in mxus]
    refs = [tile[0]] * pieces + [tile[1]] * pieces
    refs += [pltpu.ACC(q)((rest, TILE), F32) for q in mxus]
    refs += [pltpu.ACC(q)((early, TILE), F32) for q in mxus]
    pl.run_scoped(scoped, *refs)


def body(pred_input, proj_weight, proj_bias, targets, block_masks):
    images, patches, width = pred_input.shape
    feat = targets.shape[2]
    rows = proj_weight.shape[0]
    blocks = block_masks.shape[1]
    ndp, nmp = lax.axis_size("dp"), lax.axis_size("mp")
    ntot = ndp * nmp
    featp = pad_to(feat, LANES)
    groups = images // GROUP
    halves, parts = patches // LANES, width // LANES
    early = LANES
    rest = feat - early
    dma = pltpu.SemaphoreType.DMA
    vmem = pl.BlockSpec(memory_space=pltpu.VMEM)
    hbm = pl.BlockSpec(memory_space=pl.ANY)
    _, _, late_at, total_rows = layout(rows)
    inner_dp = 2
    outer_dp = ndp // inner_dp
    exchange = []
    for n in (late_at, total_rows - late_at):
        exchange += [
            pltpu.VMEM((inner_dp, outer_dp, n, LANES), F32),
            pltpu.VMEM((outer_dp, n, LANES), F32),
            pltpu.VMEM((outer_dp - 1, n, LANES), F32),
            pltpu.VMEM((outer_dp - 1, n, LANES), F32),
        ]
    exchange_sems = [dma((outer_dp,)), dma((outer_dp,)), dma((outer_dp - 1,)), dma((outer_dp - 1,))]
    summed, final = pl.pallas_call(
        functools.partial(kernel, ndp, nmp),
        out_shape=(
            jax.ShapeDtypeStruct((total_rows, LANES), F32),
            jax.ShapeDtypeStruct((1, LANES), F32),
        ),
        in_specs=[hbm, vmem, vmem, hbm, hbm],
        out_specs=(vmem,) * 2,
        scratch_shapes=[
            pltpu.VMEM((parts, images * patches, LANES), BF16),
            pltpu.VMEM((images, halves, feat, LANES), BF16),
            pltpu.VMEM((images, blocks, patches), jnp.int32),
            pltpu.VMEM((ndp - 1, rows, feat), BF16),
            pltpu.VMEM((width, featp), F32),
            pltpu.VMEM((feat, pad_to(width, TILE)), BF16),
            pltpu.VMEM((patches, LANES), BF16),
            pltpu.VMEM((featp, LANES), F32),
            pltpu.VMEM((8, featp), F32),
            pltpu.VMEM((groups, 2 * GROUP, patches), F32),
            pltpu.VMEM((nmp - 1, groups, 2 * GROUP, patches), F32),
            pltpu.VMEM((images, patches), F32),
            pltpu.VMEM((images, patches), F32),
            pltpu.VMEM((images, patches), F32),
            pltpu.VMEM((PAIR, feat, patches), F32),
            pltpu.VMEM((PAIR, feat, patches), F32),
            pltpu.VMEM((rest, PAIR * patches), BF16),
            pltpu.VMEM((rest, PAIR * patches), BF16),
            pltpu.VMEM((images, halves, early, LANES), BF16),
            pltpu.VMEM((pad_to(rest, LANES), width), F32),
            pltpu.VMEM((early, width), F32),
            pltpu.VMEM((featp, LANES), F32),
            pltpu.VMEM((CHUNK, LANES), F32),
        ] + exchange + [
            pltpu.VMEM((1, LANES), F32),
            pltpu.VMEM((ntot - 1, 1, LANES), F32),
            dma((parts, groups)), dma((halves, groups)), dma(()),
            dma((ndp - 1,)), dma((ndp - 1,)),
            dma((nmp - 1, groups)), dma((nmp - 1, groups)),
        ] + exchange_sems * 2 + [
            dma((ntot - 1,)), dma((ntot - 1,)),
        ],
        compiler_params=pltpu.CompilerParams(
            collective_id=0, has_side_effects=True, vmem_limit_bytes=60 * 1024 * 1024
        ),
    )(
        pred_input.reshape(images * patches, width),
        proj_weight,
        proj_bias,
        jnp.swapaxes(targets, 1, 2),
        block_masks,
    )
    loss, clip, gw, gb = pl.pallas_call(
        functools.partial(finish, ndp, nmp),
        out_shape=(
            jax.ShapeDtypeStruct((1, 1), F32),
            jax.ShapeDtypeStruct((1, 1), F32),
            jax.ShapeDtypeStruct((rows, feat), F32),
            jax.ShapeDtypeStruct((feat,), F32),
        ),
        in_specs=[vmem] * 2,
        out_specs=(vmem,) * 4,
    )(summed, final)
    return loss.reshape(()), clip.reshape(()), gw, gb


def solution(mesh):
    in_specs = (
        P("dp", None, None),
        P("dp", "mp"),
        P("mp"),
        P("dp", None, "mp"),
        P("dp", None, None),
    )
    out_specs = (P(), P(), P("dp", "mp"), P("mp"))
    return jax.shard_map(body, mesh=mesh, in_specs=in_specs, out_specs=out_specs, check_vma=False)
```

time: 53.9 us -> 46.9 us (0.87)
  Pallas kernels: 53 us -> 46 us
    pallas_call x1, Pallas kernels: 51.4 us -> 44.4 us  [body(): pl.pallas_call(functools.partial(kernel, ndp, nmp), out_shape=(jax.ShapeD...]
where the time goes in v1:
time: 46.9 us; the launch traced here: 46.7 us
  Pallas kernels  46 us (98%)
  between operations  0.64 us (1%)
    pallas_call x1, Pallas kernels, body(): pl.pallas_call(functools.partial(kernel, ndp, nmp), out_shape=(jax.ShapeD...  44.4 us
    pallas_call x1, Pallas kernels, body(): pl.pallas_call(functools.partial(finish, ndp, nmp), out_shape=(jax.ShapeD...  1.64 us

profile of v1, /device:TPU:0, one launch (start us, length us, event | category | flops | bytes accessed | tf_op | source)
XLA Modules:
  0.0 46.7 jit_solution(14389273582838491840)
XLA Ops:
  0.6 44.4 %shard_map.84 = (f32[128,128]{1,0:T(8,128)}, f32[1,128]{1,0:T(1,128)}) custom-call(bf16[16384,384]{1,0:T(8,128)(2,1)} %bitcast.4, bf16[48,320]{1,0:T(8,128)(2,1)} %w_ref.1, f32[320]{0:T(512)} %b_ref.1, bf16[64,320,256]{2,1,0:T(8,128)(2,1)} %bitcast.5, s32[64,4,256]{2,1,0:T(4,128)} %m_hbm.1), custom_call_target="tpu_custom_call" | custom-call | tf_op jit(solution)/shard_map/pallas_call | solution.py:506
  45.0 1.6 %shard_map.85 = (f32[1,1]{1,0:T(1,128)}, f32[1,1]{1,0:T(1,128)}, f32[48,320]{1,0:T(8,128)}, f32[320]{0:T(512)}) custom-call(f32[128,128]{1,0:T(8,128)} %get-tuple-element.10.sum_ref, f32[1,128]{1,0:T(1,128)} %get-tuple-element.11.fin_ref), custom_call_target="tpu_custom_call" | custom-call | tf_op jit(solution)/shard_map/pallas_call | solution.py:557

commit v2 on v1

--- a/solution.py
+++ b/solution.py
@@ -17,6 +17,7 @@
 TILE = 256
 ROWS = 32
 SWEEP = 16
+HAND = 5
 
 
 def pad_to(n, m):
@@ -30,12 +31,12 @@
     return half, sums, late, late + pad_to(rows, 8)
 
 
-def finish(ndp, nmp, sum_ref, fin_ref, loss_ref, clip_ref, gw_ref, gb_ref):
+def finish(ndp, nmp, sum_ref, loss_ref, clip_ref, gw_ref, gb_ref):
     rows, feat = gw_ref.shape
-    half_at, sums_at, late_at, _ = layout(rows)
+    half_at, sums_at, late_at, fin_at = layout(rows)
     tiles = pad_to(feat, LANES) // LANES
     count = sum_ref[sums_at + tiles + 1:sums_at + tiles + 2, 0:1]
-    square, loss = fin_ref[:, 0:1], fin_ref[:, 1:2]
+    square, loss = sum_ref[fin_at:fin_at + 1, 0:1], sum_ref[fin_at:fin_at + 1, 1:2]
     norm = jnp.sqrt(square) / count
     scale = jnp.minimum(1.0, 1.0 / (norm + 1e-06))
     factor = scale / count
@@ -53,12 +54,12 @@
         gb_ref[n * LANES:stop] = bias[0, :stop - n * LANES]
 
 
-def kernel(ndp, nmp, x_hbm, w_ref, b_ref, t_hbm, m_hbm,
-           out_ref, fin_ref,
-           xv, tv, mv, wall, wfull, wt, ones, bcol, brow, ssend, srecv, rbuf, mbuf, cbuf,
+def kernel(ndp, nmp, x_hbm, w_hbm, b_hbm, t_hbm, m_hbm,
+           out_hbm,
+           xv, tv, mv, w_ref, b_ref, outv, wall, wfull, wt, ones, bcol, brow, ssend, srecv, rbuf, mbuf, cbuf,
            pa, pb, sa, sb, s2, acc1, acc2, gacc, lacc,
            gs1, pv1, gm1, gr1, gs2, pv2, gm2, gr2, fsend, frecv,
-           xsem, tsem, msem, wss, wrs, sss, srs, ps1, pr1, g1s, g1r, ps2, pr2, g2s, g2r, fss, frs):
+           xsem, tsem, msem, bsem, osem, wss, wrs, whs, whr, sss, srs, ps1, pr1, g1s, g1r, ps2, pr2, g2s, g2r, fss, frs):
     images, halves, feat, _ = tv.shape
     patches = halves * LANES
     parts, _, _ = xv.shape
@@ -85,33 +86,69 @@
 
         def t_copy(g, h):
             s = pl.ds(g * GROUP, GROUP)
-            return pltpu.make_async_copy(t_hbm.at[s, :, pl.ds(h * LANES, LANES)], tv.at[s, h], tsem.at[h, g])
+            return pltpu.make_async_copy(t_hbm.at[s, :, pl.ds(h * LANES, LANES)], tv.at[s, h], tsem.at[g])
 
         def x_copy(g, j):
             s = pl.ds(g * GROUP * patches, GROUP * patches)
-            return pltpu.make_async_copy(x_hbm.at[s, pl.ds(j * LANES, LANES)], xv.at[j, s], xsem.at[j, g])
+            return pltpu.make_async_copy(x_hbm.at[s, pl.ds(j * LANES, LANES)], xv.at[j, s], xsem.at[g])
 
         def x_start(g):
             for j in range(parts):
                 x_copy(g, j).start()
 
+        def arrive(ref, sem):
+            pltpu.make_async_copy(ref, ref, sem).wait()
+
         def x_wait(g):
-            for j in range(parts):
-                x_copy(g, j).wait()
-
-        m_copy = pltpu.make_async_copy(m_hbm, mv, msem)
+            arrive(xv.at[:, pl.ds(g * GROUP * patches, GROUP * patches)], xsem.at[g])
+
+        m_copy = pltpu.make_async_copy(m_hbm, mv, msem.at[0])
+        w_own = pltpu.make_async_copy(w_hbm, w_ref, msem.at[1])
+        b_own = pltpu.make_async_copy(b_hbm, b_ref, bsem)
         barrier = pltpu.get_barrier_semaphore()
 
-        def greet(o, _):
-            d = lax.rem(me + o, ntot)
-            pl.semaphore_signal(barrier, inc=1, device_id=(d // nmp, lax.rem(d, nmp)), device_id_type=MESH)
-            return 0
-
-        lax.fori_loop(1, ntot, greet, 0)
+        other = 1 - near
+
+        def line(o):
+            return lax.rem(far + o, outer_dp) * inner_dp + near
+
+        partner = far * inner_dp + other
+        peers = [(line(o), mp) for o in range(1, outer_dp)] + [(partner, mp)]
+        peers += [(dp, lax.rem(mp + o, nmp)) for o in range(1, nmp)]
+        for peer in peers:
+            pl.semaphore_signal(barrier, inc=1, device_id=peer, device_id_type=MESH)
+        w_own.start()
+        b_own.start()
         m_copy.start()
         for g in range(groups):
             for h in range(halves):
                 t_copy(g, h).start()
+
+        pl.semaphore_wait(barrier, len(peers))
+
+        def w_copy(o):
+            return pltpu.make_async_remote_copy(
+                src_ref=w_ref, dst_ref=wall.at[dp], send_sem=wss, recv_sem=wrs.at[o],
+                device_id=(line(o), mp), device_id_type=MESH)
+
+        def w_hand(o):
+            src = lax.rem(far - o + outer_dp, outer_dp) * inner_dp + near
+            own = isinstance(o, int) and o == 0
+            return pltpu.make_async_remote_copy(
+                src_ref=w_ref if own else wall.at[src], dst_ref=wall.at[src], send_sem=whs, recv_sem=whr,
+                device_id=(partner, mp), device_id_type=MESH)
+
+        def ranked(offset, n):
+            picks = 0
+            for f in range(outer_dp):
+                near_first = sorted(range(1, outer_dp), key=lambda o: abs((f + offset * o) % outer_dp - f))
+                picks = picks + jnp.where(far == f, near_first[n], 0)
+            return picks
+
+        w_own.wait()
+        for n in reversed(range(outer_dp - 1)):
+            w_copy(ranked(1, n)).start()
+        w_hand(0).start()
 
         gacc[...] = jnp.zeros_like(gacc)
         lacc[...] = jnp.zeros_like(lacc)
@@ -124,6 +161,7 @@
             gs2[...] = jnp.zeros_like(gs2)
         lane = lax.broadcasted_iota(jnp.int32, ones.shape, 1)
         ones[...] = jnp.where(lane < 3, 1.0, 0.0).astype(BF16)
+        b_own.wait()
         brow[0:1, :feat] = b_ref[...].reshape(1, feat)
         bcol[...] = jnp.transpose(jnp.broadcast_to(brow[0:1, :], (LANES, featp)))
         bias = bcol[:feat, :]
@@ -141,20 +179,10 @@
             for ref in proj[q] + [grad_acc[q], late_acc[q]]:
                 pltpu.matmul_pop(ref)
 
-        pl.semaphore_wait(barrier, ntot - 1)
-
-        def w_copy(o):
-            return pltpu.make_async_remote_copy(
-                src_ref=w_ref, dst_ref=wall.at[o - 1], send_sem=wss.at[o - 1], recv_sem=wrs.at[o - 1],
-                device_id=(lax.rem(dp + o, ndp), mp), device_id_type=MESH)
-
-        for o in range(1, ndp):
-            w_copy(o).start()
-
         def s_copy(o, g):
             return pltpu.make_async_remote_copy(
                 src_ref=ssend.at[g], dst_ref=srecv.at[o - 1, g],
-                send_sem=sss.at[o - 1, g], recv_sem=srs.at[o - 1, g],
+                send_sem=sss, recv_sem=srs.at[g],
                 device_id=(dp, lax.rem(mp + o, nmp)), device_id_type=MESH)
 
         m_copy.wait()
@@ -167,8 +195,7 @@
         lax.fori_loop(0, groups, cover, 0)
 
         def stats(g, _):
-            for h in range(halves):
-                t_copy(g, h).wait()
+            arrive(tv.at[pl.ds(g * GROUP, GROUP)], tsem.at[g])
 
             @pl.when(g >= 2)
             def _():
@@ -198,21 +225,29 @@
                 for o in range(1, nmp):
                     s_copy(o, g - 1).start()
 
+            @pl.when(g == HAND)
+            def _():
+                hand_over(0)
+
             return 0
+
+        def hand_over(n):
+            o = ranked(-1, n)
+            w_copy(o).wait_recv()
+            w_hand(o).start()
 
         lax.fori_loop(0, groups, stats, 0)
         for g in range(groups - 2, groups):
             x_start(g)
 
-        for o in range(1, ndp):
-            w_copy(o).wait_recv()
         for o in range(1, nmp):
             s_copy(o, groups - 1).start()
+        for n in range(1, outer_dp - 1):
+            hand_over(n)
+        wall[dp] = w_ref[...]
+        arrive(wall.at[pl.ds(0, outer_dp)], whr)
         for k in range(ndp):
-            slot = lax.rem(dp - k + ndp, ndp)
-            other = wall[jnp.maximum(slot - 1, 0)].astype(F32)
-            block = jnp.where(slot == 0, w_ref[...].astype(F32), other)
-            wfull[k * rows:(k + 1) * rows, :feat] = block
+            wfull[k * rows:(k + 1) * rows, :feat] = wall[k].astype(F32)
         wt[:, :width] = jnp.transpose(wfull[...])[:feat].astype(BF16)
 
         def x_tile(img, part):
@@ -305,8 +340,7 @@
             def _():
                 x_wait(g + 1)
 
-            for o in range(1, nmp):
-                s_copy(o, g).wait_recv()
+            arrive(srecv.at[:, g], srs.at[g])
             parts_in = [ssend[g]] + [srecv[o - 1, g] for o in range(1, nmp)]
             sums = [p[:GROUP] for p in parts_in]
             mean = functools.reduce(jnp.add, sums) * (1.0 / feat_full)
@@ -358,21 +392,18 @@
                 [mine[:rows // 2, LANES:LANES + half], mine[rows // 2:, LANES:LANES + half]], axis=1)
             slot[sums_at:, :] = extra
 
-        other = 1 - near
-
         def p_copy(o, bufs):
             src, dst, _, _, ss, rs, _, _ = bufs
             to = lax.rem(far + o, outer_dp)
             return pltpu.make_async_remote_copy(
-                src_ref=src.at[other, to], dst_ref=dst.at[o], send_sem=ss.at[o], recv_sem=rs.at[o],
-                device_id=(far * inner_dp + other, mp), device_id_type=MESH)
+                src_ref=src.at[other, to], dst_ref=dst.at[o], send_sem=ss, recv_sem=rs.at[o],
+                device_id=(partner, mp), device_id_type=MESH)
 
         def g_copy(o, bufs):
             _, _, src, dst, _, _, ss, rs = bufs
-            to = lax.rem(far + o, outer_dp)
             return pltpu.make_async_remote_copy(
-                src_ref=src.at[o - 1], dst_ref=dst.at[o - 1], send_sem=ss.at[o - 1], recv_sem=rs.at[o - 1],
-                device_id=(to * inner_dp + near, mp), device_id_type=MESH)
+                src_ref=src.at[o - 1], dst_ref=dst.at[o - 1], send_sem=ss, recv_sem=rs,
+                device_id=(line(o), mp), device_id_type=MESH)
 
         first = (gs1, pv1, gm1, gr1, ps1, pr1, g1s, g1r)
         second = (gs2, pv2, gm2, gr2, ps2, pr2, g2s, g2r)
@@ -418,11 +449,11 @@
                     g_copy(o, bufs).start()
             pairs.append(pair)
         for n, bufs in enumerate((first, second)):
+            arrive(bufs[3], bufs[7])
             for o in range(1, outer_dp):
-                g_copy(o, bufs).wait_recv()
                 pairs[n] = pairs[n] + bufs[3][o - 1]
-        out_ref[:late_at, :] = pairs[0]
-        out_ref[late_at:, :] = pairs[1]
+        outv[:late_at, :] = pairs[0]
+        outv[late_at:total_rows, :] = pairs[1]
         head = pairs[0][:sums_at]
         sums = pairs[0][sums_at:]
         bias_grad = sums[:tiles]
@@ -431,43 +462,34 @@
         lane = lax.broadcasted_iota(jnp.int32, (1, LANES), 1)
         fsend[...] = jnp.where(lane == 0, square + bias_square * (1.0 / ndp), sums[tiles:tiles + 1, :])
 
-        def f_copy(o):
-            d = lax.rem(me + o, ntot)
+        def f_copy(d):
             return pltpu.make_async_remote_copy(
-                src_ref=fsend, dst_ref=frecv.at[o - 1], send_sem=fss.at[o - 1], recv_sem=frs.at[o - 1],
+                src_ref=fsend, dst_ref=frecv.at[me], send_sem=fss, recv_sem=frs,
                 device_id=(d // nmp, lax.rem(d, nmp)), device_id_type=MESH)
 
         def f_start(o, _):
-            f_copy(o).start()
+            f_copy(o + jnp.where(o >= me, 1, 0)).start()
             return 0
 
-        def f_wait(o, _):
-            f_copy(o).wait_recv()
-            return 0
-
-        lax.fori_loop(1, ntot, f_start, 0)
-
-        for o in range(1, ndp):
-            w_copy(o).wait_send()
+        lax.fori_loop(0, ntot - 1, f_start, 0)
+        frecv[me] = fsend[...]
+        body_out = pltpu.make_async_copy(outv.at[pl.ds(0, total_rows)], out_hbm.at[pl.ds(0, total_rows)], osem.at[0])
+        body_out.start()
+        tail_out = pltpu.make_async_copy(outv.at[pl.ds(total_rows, 8)], out_hbm.at[pl.ds(total_rows, 8)], osem.at[1])
+
+        arrive(wall.at[pl.ds(0, outer_dp - 1)], wss)
+        arrive(wall.at[pl.ds(0, outer_dp)], whs)
         for bufs in (first, second):
-            for o in order:
-                p_copy(o, bufs).wait_send()
-                if o:
-                    g_copy(o, bufs).wait_send()
-
-        def s_drain(g, _):
-            for o in range(1, nmp):
-                s_copy(o, g).wait_send()
-            return 0
-
-        def f_drain(o, _):
-            f_copy(o).wait_send()
-            return 0
-
-        lax.fori_loop(0, groups, s_drain, 0)
-        lax.fori_loop(1, ntot, f_wait, 0)
-        fin_ref[...] = fsend[...] + jnp.sum(frecv[...], axis=0)
-        lax.fori_loop(1, ntot, f_drain, 0)
+            arrive(bufs[0].at[0], bufs[4])
+            arrive(bufs[2], bufs[6])
+        arrive(srecv, sss)
+        body_out.wait()
+        everyone = frecv.at[pl.ds(0, ntot - 1)]
+        arrive(everyone, frs)
+        outv[total_rows:, :] = jnp.broadcast_to(jnp.sum(frecv[...], axis=0), (8, LANES))
+        tail_out.start()
+        arrive(everyone, fss)
+        tail_out.wait()
 
     tile = [pltpu.ACC(q)((ROWS, TILE), F32) for q in mxus]
     refs = [tile[0]] * pieces + [tile[1]] * pieces
@@ -502,20 +524,20 @@
             pltpu.VMEM((outer_dp - 1, n, LANES), F32),
             pltpu.VMEM((outer_dp - 1, n, LANES), F32),
         ]
-    exchange_sems = [dma((outer_dp,)), dma((outer_dp,)), dma((outer_dp - 1,)), dma((outer_dp - 1,))]
-    summed, final = pl.pallas_call(
+    exchange_sems = [dma(()), dma((outer_dp,)), dma(()), dma(())]
+    summed = pl.pallas_call(
         functools.partial(kernel, ndp, nmp),
-        out_shape=(
-            jax.ShapeDtypeStruct((total_rows, LANES), F32),
-            jax.ShapeDtypeStruct((1, LANES), F32),
-        ),
-        in_specs=[hbm, vmem, vmem, hbm, hbm],
-        out_specs=(vmem,) * 2,
+        out_shape=jax.ShapeDtypeStruct((total_rows + 8, LANES), F32),
+        in_specs=[hbm] * 5,
+        out_specs=hbm,
         scratch_shapes=[
             pltpu.VMEM((parts, images * patches, LANES), BF16),
             pltpu.VMEM((images, halves, feat, LANES), BF16),
             pltpu.VMEM((images, blocks, patches), jnp.int32),
-            pltpu.VMEM((ndp - 1, rows, feat), BF16),
+            pltpu.VMEM((rows, feat), BF16),
+            pltpu.VMEM((feat,), F32),
+            pltpu.VMEM((total_rows + 8, LANES), F32),
+            pltpu.VMEM((ndp, rows, feat), BF16),
             pltpu.VMEM((width, featp), F32),
             pltpu.VMEM((feat, pad_to(width, TILE)), BF16),
             pltpu.VMEM((patches, LANES), BF16),
@@ -537,13 +559,10 @@
             pltpu.VMEM((CHUNK, LANES), F32),
         ] + exchange + [
             pltpu.VMEM((1, LANES), F32),
-            pltpu.VMEM((ntot - 1, 1, LANES), F32),
-            dma((parts, groups)), dma((halves, groups)), dma(()),
-            dma((ndp - 1,)), dma((ndp - 1,)),
-            dma((nmp - 1, groups)), dma((nmp - 1, groups)),
-        ] + exchange_sems * 2 + [
-            dma((ntot - 1,)), dma((ntot - 1,)),
-        ],
+            pltpu.VMEM((ntot, 1, LANES), F32),
+            dma((groups,)), dma((groups,)), dma((2,)), dma(()), dma((2,)),
+            dma(()), dma((outer_dp,)), dma(()), dma(()), dma(()), dma((groups,)),
+        ] + exchange_sems * 2 + [dma(()), dma(())],
         compiler_params=pltpu.CompilerParams(
             collective_id=0, has_side_effects=True, vmem_limit_bytes=60 * 1024 * 1024
         ),
@@ -562,9 +581,9 @@
             jax.ShapeDtypeStruct((rows, feat), F32),
             jax.ShapeDtypeStruct((feat,), F32),
         ),
-        in_specs=[vmem] * 2,
+        in_specs=[vmem],
         out_specs=(vmem,) * 4,
-    )(summed, final)
+    )(summed)
     return loss.reshape(()), clip.reshape(()), gw, gb
 
 

time: 46.9 us -> 44.1 us (0.940)
  Pallas kernels: 46 us -> 43.3 us
    pallas_call x1, Pallas kernels: 44.4 us -> 41.6 us  [body(): pl.pallas_call(functools.partial(kernel, ndp, nmp), out_shape=jax.ShapeDt...]
where the time goes in v2:
time: 44.1 us; the launch traced here: 43.9 us
  Pallas kernels  43.3 us (98%)
  between operations  0.64 us (1%)
    pallas_call x1, Pallas kernels, body(): pl.pallas_call(functools.partial(kernel, ndp, nmp), out_shape=jax.ShapeDt...  41.6 us
    pallas_call x1, Pallas kernels, body(): pl.pallas_call(functools.partial(finish, ndp, nmp), out_shape=(jax.ShapeD...  1.67 us

profile of v2, /device:TPU:0, one launch (start us, length us, event | category | flops | bytes accessed | tf_op | source)
XLA Modules:
  0.0 43.9 jit_solution(13205521051055234050)
XLA Ops:
  0.6 41.6 %shard_map.84.sum_ref = f32[136,128]{1,0:T(8,128)} custom-call(bf16[16384,384]{1,0:T(8,128)(2,1)} %bitcast.4, bf16[48,320]{1,0:T(8,128)(2,1)} %w_hbm.1, f32[320]{0:T(512)} %b_hbm.1, bf16[64,320,256]{2,1,0:T(8,128)(2,1)} %bitcast.5, s32[64,4,256]{2,1,0:T(4,128)} %m_hbm.1), custom_call_target="tpu_custom_call" | custom-call | tf_op jit(solution)/shard_map/pallas_call | solution.py:528
  42.2 1.7 %shard_map.85 = (f32[1,1]{1,0:T(1,128)}, f32[1,1]{1,0:T(1,128)}, f32[48,320]{1,0:T(8,128)}, f32[320]{0:T(512)}) custom-call(f32[136,128]{1,0:T(8,128)} %shard_map.84.sum_ref), custom_call_target="tpu_custom_call" | custom-call | tf_op jit(solution)/shard_map/pallas_call | solution.py:576

commit v3 on v2

--- a/solution.py
+++ b/solution.py
@@ -17,7 +17,7 @@
 TILE = 256
 ROWS = 32
 SWEEP = 16
-HAND = 5
+HANDS = (3, 5, 7)
 
 
 def pad_to(n, m):
@@ -55,11 +55,11 @@
 
 
 def kernel(ndp, nmp, x_hbm, w_hbm, b_hbm, t_hbm, m_hbm,
-           out_hbm,
-           xv, tv, mv, w_ref, b_ref, outv, wall, wfull, wt, ones, bcol, brow, ssend, srecv, rbuf, mbuf, cbuf,
+           outv,
+           xv, tv, mv, w_ref, b_ref, wall, wfull, wt, ones, bcol, brow, ssend, srecv, rbuf, mbuf, cbuf,
            pa, pb, sa, sb, s2, acc1, acc2, gacc, lacc,
            gs1, pv1, gm1, gr1, gs2, pv2, gm2, gr2, fsend, frecv,
-           xsem, tsem, msem, bsem, osem, wss, wrs, whs, whr, sss, srs, ps1, pr1, g1s, g1r, ps2, pr2, g2s, g2r, fss, frs):
+           xsem, tsem, msem, bsem, wss, wrs, whs, whr, sss, srs, ps1, pr1, g1s, g1r, ps2, pr2, g2s, g2r, fss, frs):
     images, halves, feat, _ = tv.shape
     patches = halves * LANES
     parts, _, _ = xv.shape
@@ -179,6 +179,17 @@
             for ref in proj[q] + [grad_acc[q], late_acc[q]]:
                 pltpu.matmul_pop(ref)
 
+        def x_tile(img, part):
+            at = pl.ds(pl.multiple_of(img * patches, patches), patches)
+            left = xv[2 * part, at, :]
+            right = xv[2 * part + 1, at, :] if 2 * part + 1 < parts else ones[...]
+            return jnp.concatenate([left, right], axis=1)
+
+        def push_project(k, part):
+            for q in mxus:
+                tile = x_tile(PAIR * k + q, part)
+                pltpu.matmul_push_rhs(tile, staging_register=part, mxu_index=q, transpose=True)
+
         def s_copy(o, g):
             return pltpu.make_async_remote_copy(
                 src_ref=ssend.at[g], dst_ref=srecv.at[o - 1, g],
@@ -225,9 +236,8 @@
                 for o in range(1, nmp):
                     s_copy(o, g - 1).start()
 
-            @pl.when(g == HAND)
-            def _():
-                hand_over(0)
+            for n in range(min(outer_dp - 1, len(HANDS))):
+                pl.when(g == HANDS[n])(functools.partial(hand_over, n))
 
             return 0
 
@@ -242,24 +252,16 @@
 
         for o in range(1, nmp):
             s_copy(o, groups - 1).start()
-        for n in range(1, outer_dp - 1):
+        for n in range(len(HANDS), outer_dp - 1):
             hand_over(n)
+        x_wait(0)
+        for part in range(2):
+            push_project(0, part)
         wall[dp] = w_ref[...]
         arrive(wall.at[pl.ds(0, outer_dp)], whr)
         for k in range(ndp):
             wfull[k * rows:(k + 1) * rows, :feat] = wall[k].astype(F32)
         wt[:, :width] = jnp.transpose(wfull[...])[:feat].astype(BF16)
-
-        def x_tile(img, part):
-            at = pl.ds(pl.multiple_of(img * patches, patches), patches)
-            left = xv[2 * part, at, :]
-            right = xv[2 * part + 1, at, :] if 2 * part + 1 < parts else ones[...]
-            return jnp.concatenate([left, right], axis=1)
-
-        def push_project(k, part):
-            for q in mxus:
-                tile = x_tile(PAIR * k + q, part)
-                pltpu.matmul_push_rhs(tile, staging_register=part, mxu_index=q, transpose=True)
 
         def project(part, c):
             lhs = wt[c * ROWS:(c + 1) * ROWS, part * TILE:(part + 1) * TILE]
@@ -323,13 +325,9 @@
                 keep(p_out, c)
             lacc[...] += functools.reduce(jnp.add, loss)
 
-        x_wait(0)
-        push_project(0, 0)
-        for c in range(pieces):
-            project(0, c)
-        push_project(0, 1)
-        for c in range(pieces):
-            project(1, c)
+        for part in range(2):
+            for c in range(pieces):
+                project(part, c)
         push_project(1, 0)
         for c in range(pieces):
             keep(pa, c)
@@ -407,7 +405,7 @@
 
         first = (gs1, pv1, gm1, gr1, ps1, pr1, g1s, g1r)
         second = (gs2, pv2, gm2, gr2, ps2, pr2, g2s, g2r)
-        order = list(range(1, outer_dp)) + [0]
+        order = [ranked(1, n) for n in reversed(range(outer_dp - 1))] + [0]
         for o in order:
             p_copy(o, first).start()
 
@@ -444,7 +442,7 @@
             for o in order:
                 p_copy(o, bufs).wait_recv()
                 pair = src[near, lax.rem(far + o, outer_dp)] + dst[o]
-                if o:
+                if o is not order[-1]:
                     mid_buf[o - 1] = pair
                     g_copy(o, bufs).start()
             pairs.append(pair)
@@ -473,23 +471,16 @@
 
         lax.fori_loop(0, ntot - 1, f_start, 0)
         frecv[me] = fsend[...]
-        body_out = pltpu.make_async_copy(outv.at[pl.ds(0, total_rows)], out_hbm.at[pl.ds(0, total_rows)], osem.at[0])
-        body_out.start()
-        tail_out = pltpu.make_async_copy(outv.at[pl.ds(total_rows, 8)], out_hbm.at[pl.ds(total_rows, 8)], osem.at[1])
-
         arrive(wall.at[pl.ds(0, outer_dp - 1)], wss)
         arrive(wall.at[pl.ds(0, outer_dp)], whs)
         for bufs in (first, second):
             arrive(bufs[0].at[0], bufs[4])
             arrive(bufs[2], bufs[6])
         arrive(srecv, sss)
-        body_out.wait()
         everyone = frecv.at[pl.ds(0, ntot - 1)]
         arrive(everyone, frs)
         outv[total_rows:, :] = jnp.broadcast_to(jnp.sum(frecv[...], axis=0), (8, LANES))
-        tail_out.start()
         arrive(everyone, fss)
-        tail_out.wait()
 
     tile = [pltpu.ACC(q)((ROWS, TILE), F32) for q in mxus]
     refs = [tile[0]] * pieces + [tile[1]] * pieces
@@ -527,16 +518,15 @@
     exchange_sems = [dma(()), dma((outer_dp,)), dma(()), dma(())]
     summed = pl.pallas_call(
         functools.partial(kernel, ndp, nmp),
-        out_shape=jax.ShapeDtypeStruct((total_rows + 8, LANES), F32),
+        out_shape=pltpu.VMEM((total_rows + 8, LANES), F32),
         in_specs=[hbm] * 5,
-        out_specs=hbm,
+        out_specs=vmem,
         scratch_shapes=[
             pltpu.VMEM((parts, images * patches, LANES), BF16),
             pltpu.VMEM((images, halves, feat, LANES), BF16),
             pltpu.VMEM((images, blocks, patches), jnp.int32),
             pltpu.VMEM((rows, feat), BF16),
             pltpu.VMEM((feat,), F32),
-            pltpu.VMEM((total_rows + 8, LANES), F32),
             pltpu.VMEM((ndp, rows, feat), BF16),
             pltpu.VMEM((width, featp), F32),
             pltpu.VMEM((feat, pad_to(width, TILE)), BF16),
@@ -560,7 +550,7 @@
         ] + exchange + [
             pltpu.VMEM((1, LANES), F32),
             pltpu.VMEM((ntot, 1, LANES), F32),
-            dma((groups,)), dma((groups,)), dma((2,)), dma(()), dma((2,)),
+            dma((groups,)), dma((groups,)), dma((2,)), dma(()),
             dma(()), dma((outer_dp,)), dma(()), dma(()), dma(()), dma((groups,)),
         ] + exchange_sems * 2 + [dma(()), dma(())],
         compiler_params=pltpu.CompilerParams(
@@ -583,7 +573,7 @@
         ),
         in_specs=[vmem],
         out_specs=(vmem,) * 4,
-    )(summed)
+    )(pltpu.with_memory_space_constraint(summed, pltpu.VMEM))
     return loss.reshape(()), clip.reshape(()), gw, gb
 
 

time: 44.1 us -> 42.5 us (0.964)
  Pallas kernels: 43.3 us -> 41.7 us
    pallas_call x1, Pallas kernels: 1.67 us -> 0.78 us  [body(): pl.pallas_call(functools.partial(finish, ndp, nmp), out_shape=(jax.ShapeD...]
    pallas_call x1, Pallas kernels: 41.6 us -> 40.9 us  [body(): pl.pallas_call(functools.partial(kernel, ndp, nmp), out_shape=pltpu.VMEM(...]
where the time goes in v3:
time: 42.5 us; the launch traced here: 42.3 us
  Pallas kernels  41.7 us (98%)
  between operations  0.64 us (2%)
    pallas_call x1, Pallas kernels, body(): pl.pallas_call(functools.partial(kernel, ndp, nmp), out_shape=pltpu.VMEM(...  40.9 us

profile of v3, /device:TPU:0, one launch (start us, length us, event | category | flops | bytes accessed | tf_op | source)
XLA Modules:
  0.0 42.3 jit_solution(4479855152853922124)
XLA Ops:
  0.6 40.9 %shard_map.84.sum_ref = f32[136,128]{1,0:T(8,128)S(1)} custom-call(bf16[16384,384]{1,0:T(8,128)(2,1)} %bitcast.4, bf16[48,320]{1,0:T(8,128)(2,1)} %w_hbm.1, f32[320]{0:T(512)} %b_hbm.1, bf16[64,320,256]{2,1,0:T(8,128)(2,1)} %bitcast.5, s32[64,4,256]{2,1,0:T(4,128)} %m_hbm.1), custom_call_target="tpu_custom_call" | custom-call | tf_op jit(solution)/shard_map/pallas_call | solution.py:519
  41.5 0.8 %shard_map.85 = (f32[1,1]{1,0:T(1,128)}, f32[1,1]{1,0:T(1,128)}, f32[48,320]{1,0:T(8,128)}, f32[320]{0:T(512)}) custom-call(f32[136,128]{1,0:T(8,128)S(1)} %shard_map.84.sum_ref), custom_call_target="tpu_custom_call" | custom-call | tf_op jit(solution)/shard_map/pallas_call | solution.py:566

commit v4 on v3

--- a/solution.py
+++ b/solution.py
@@ -17,7 +17,7 @@
 TILE = 256
 ROWS = 32
 SWEEP = 16
-HANDS = (3, 5, 7)
+HANDS = (6, 7)
 
 
 def pad_to(n, m):
@@ -150,6 +150,73 @@
             w_copy(ranked(1, n)).start()
         w_hand(0).start()
 
+        def x_tile(img, part):
+            at = pl.ds(pl.multiple_of(img * patches, patches), patches)
+            left = xv[2 * part, at, :]
+            right = xv[2 * part + 1, at, :] if 2 * part + 1 < parts else ones[...]
+            return jnp.concatenate([left, right], axis=1)
+
+        def push_project(k, part):
+            for q in mxus:
+                tile = x_tile(PAIR * k + q, part)
+                pltpu.matmul_push_rhs(tile, staging_register=part, mxu_index=q, transpose=True)
+
+        def s_copy(o, g):
+            return pltpu.make_async_remote_copy(
+                src_ref=ssend.at[g], dst_ref=srecv.at[o - 1, g],
+                send_sem=sss, recv_sem=srs.at[g],
+                device_id=(dp, lax.rem(mp + o, nmp)), device_id_type=MESH)
+
+        def stats(g, _):
+            arrive(tv.at[pl.ds(g * GROUP, GROUP)], tsem.at[g])
+
+            @pl.when(g >= 2)
+            def _():
+                x_start(g - 2)
+
+            sums, squares = [], []
+            for j in range(GROUP):
+                i = g * GROUP + j
+                for h in range(halves):
+                    part = jnp.zeros((CHUNK, LANES), F32)
+                    for c in range(0, feat, CHUNK):
+                        part = part + tv[i, h, c:c + CHUNK, :].astype(F32)
+                    total = jnp.sum(part, axis=0, keepdims=True)
+                    mean = total * (1.0 / feat)
+                    part = jnp.zeros((CHUNK, LANES), F32)
+                    for c in range(0, feat, CHUNK):
+                        centred = tv[i, h, c:c + CHUNK, :].astype(F32) - mean
+                        part = part + centred * centred
+                    sums.append(total)
+                    squares.append(jnp.sum(part, axis=0, keepdims=True))
+            for h in range(halves):
+                block = jnp.concatenate(sums[h::halves] + squares[h::halves], axis=0)
+                ssend[g, :, h * LANES:(h + 1) * LANES] = block
+
+            @pl.when(g > 0)
+            def _():
+                for o in range(1, nmp):
+                    s_copy(o, g - 1).start()
+
+            for n in range(min(outer_dp - 1, len(HANDS))):
+                pl.when(g == HANDS[n])(functools.partial(hand_over, n))
+
+            return 0
+
+        def hand_over(n):
+            src = n + jnp.where(n >= far, 1, 0)
+            o = lax.rem(far - src + outer_dp, outer_dp)
+            w_copy(o).wait_recv()
+            w_hand(o).start()
+
+        lax.fori_loop(0, groups, stats, 0)
+        for g in range(groups - 2, groups):
+            x_start(g)
+
+        for o in range(1, nmp):
+            s_copy(o, groups - 1).start()
+        for n in range(len(HANDS), outer_dp - 1):
+            hand_over(n)
         gacc[...] = jnp.zeros_like(gacc)
         lacc[...] = jnp.zeros_like(lacc)
         sb[...] = jnp.zeros_like(sb)
@@ -179,23 +246,6 @@
             for ref in proj[q] + [grad_acc[q], late_acc[q]]:
                 pltpu.matmul_pop(ref)
 
-        def x_tile(img, part):
-            at = pl.ds(pl.multiple_of(img * patches, patches), patches)
-            left = xv[2 * part, at, :]
-            right = xv[2 * part + 1, at, :] if 2 * part + 1 < parts else ones[...]
-            return jnp.concatenate([left, right], axis=1)
-
-        def push_project(k, part):
-            for q in mxus:
-                tile = x_tile(PAIR * k + q, part)
-                pltpu.matmul_push_rhs(tile, staging_register=part, mxu_index=q, transpose=True)
-
-        def s_copy(o, g):
-            return pltpu.make_async_remote_copy(
-                src_ref=ssend.at[g], dst_ref=srecv.at[o - 1, g],
-                send_sem=sss, recv_sem=srs.at[g],
-                device_id=(dp, lax.rem(mp + o, nmp)), device_id_type=MESH)
-
         m_copy.wait()
 
         def cover(g, _):
@@ -205,55 +255,6 @@
 
         lax.fori_loop(0, groups, cover, 0)
 
-        def stats(g, _):
-            arrive(tv.at[pl.ds(g * GROUP, GROUP)], tsem.at[g])
-
-            @pl.when(g >= 2)
-            def _():
-                x_start(g - 2)
-
-            sums, squares = [], []
-            for j in range(GROUP):
-                i = g * GROUP + j
-                for h in range(halves):
-                    part = jnp.zeros((CHUNK, LANES), F32)
-                    for c in range(0, feat, CHUNK):
-                        part = part + tv[i, h, c:c + CHUNK, :].astype(F32)
-                    total = jnp.sum(part, axis=0, keepdims=True)
-                    mean = total * (1.0 / feat)
-                    part = jnp.zeros((CHUNK, LANES), F32)
-                    for c in range(0, feat, CHUNK):
-                        centred = tv[i, h, c:c + CHUNK, :].astype(F32) - mean
-                        part = part + centred * centred
-                    sums.append(total)
-                    squares.append(jnp.sum(part, axis=0, keepdims=True))
-            for h in range(halves):
-                block = jnp.concatenate(sums[h::halves] + squares[h::halves], axis=0)
-                ssend[g, :, h * LANES:(h + 1) * LANES] = block
-
-            @pl.when(g > 0)
-            def _():
-                for o in range(1, nmp):
-                    s_copy(o, g - 1).start()
-
-            for n in range(min(outer_dp - 1, len(HANDS))):
-                pl.when(g == HANDS[n])(functools.partial(hand_over, n))
-
-            return 0
-
-        def hand_over(n):
-            o = ranked(-1, n)
-            w_copy(o).wait_recv()
-            w_hand(o).start()
-
-        lax.fori_loop(0, groups, stats, 0)
-        for g in range(groups - 2, groups):
-            x_start(g)
-
-        for o in range(1, nmp):
-            s_copy(o, groups - 1).start()
-        for n in range(len(HANDS), outer_dp - 1):
-            hand_over(n)
         x_wait(0)
         for part in range(2):
             push_project(0, part)

time: 42.5 us -> 41.2 us (0.969)
  Pallas kernels: 41.7 us -> 40.4 us
    pallas_call x1, Pallas kernels: 40.9 us -> 39.7 us  [body(): pl.pallas_call(functools.partial(kernel, ndp, nmp), out_shape=pltpu.VMEM(...]
where the time goes in v4:
time: 41.2 us; the launch traced here: 41.1 us
  Pallas kernels  40.4 us (98%)
  between operations  0.64 us (2%)
    pallas_call x1, Pallas kernels, body(): pl.pallas_call(functools.partial(kernel, ndp, nmp), out_shape=pltpu.VMEM(...  39.7 us

profile of v4, /device:TPU:0, one launch (start us, length us, event | category | flops | bytes accessed | tf_op | source)
XLA Modules:
  0.0 41.1 jit_solution(4360966041087640248)
XLA Ops:
  0.6 39.7 %shard_map.84.sum_ref = f32[136,128]{1,0:T(8,128)S(1)} custom-call(bf16[16384,384]{1,0:T(8,128)(2,1)} %bitcast.4, bf16[48,320]{1,0:T(8,128)(2,1)} %w_hbm.1, f32[320]{0:T(512)} %b_hbm.1, bf16[64,320,256]{2,1,0:T(8,128)(2,1)} %bitcast.5, s32[64,4,256]{2,1,0:T(4,128)} %m_hbm.1), custom_call_target="tpu_custom_call" | custom-call | tf_op jit(solution)/shard_map/pallas_call | solution.py:520
  40.3 0.8 %shard_map.85 = (f32[1,1]{1,0:T(1,128)}, f32[1,1]{1,0:T(1,128)}, f32[48,320]{1,0:T(8,128)}, f32[320]{0:T(512)}) custom-call(f32[136,128]{1,0:T(8,128)S(1)} %shard_map.84.sum_ref), custom_call_target="tpu_custom_call" | custom-call | tf_op jit(solution)/shard_map/pallas_call | solution.py:567

commit v5 on v4

--- a/solution.py
+++ b/solution.py
@@ -15,8 +15,8 @@
 PAIR = 2
 CHUNK = 16
 TILE = 256
-ROWS = 32
-SWEEP = 16
+ROWS = 16
+SWEEP = 32
 HANDS = (6, 7)
 
 
@@ -58,8 +58,8 @@
            outv,
            xv, tv, mv, w_ref, b_ref, wall, wfull, wt, ones, bcol, brow, ssend, srecv, rbuf, mbuf, cbuf,
            pa, pb, sa, sb, s2, acc1, acc2, gacc, lacc,
-           gs1, pv1, gm1, gr1, gs2, pv2, gm2, gr2, fsend, frecv,
-           xsem, tsem, msem, bsem, wss, wrs, whs, whr, sss, srs, ps1, pr1, g1s, g1r, ps2, pr2, g2s, g2r, fss, frs):
+           gs1, pv1, gm1, gr1, gs2, pv2, gm2, gr2, hs, hr, ht, hv, fsend, frecv,
+           xsem, tsem, msem, bsem, wss, wrs, whs, whr, sss, srs, ps1, pr1, g1s, g1r, ps2, pr2, g2s, g2r, hss, hrs, hps, hpr, fss, frs):
     images, halves, feat, _ = tv.shape
     patches = halves * LANES
     parts, _, _ = xv.shape
@@ -226,6 +226,7 @@
         if rows % 16:
             gs1[...] = jnp.zeros_like(gs1)
             gs2[...] = jnp.zeros_like(gs2)
+            hs[...] = jnp.zeros_like(hs)
         lane = lax.broadcasted_iota(jnp.int32, ones.shape, 1)
         ones[...] = jnp.where(lane < 3, 1.0, 0.0).astype(BF16)
         b_own.wait()
@@ -387,9 +388,9 @@
             slot = gs1.at[k % inner_dp, k // inner_dp]
             mine = full[k * rows:(k + 1) * rows]
             slot[:rows, :] = mine[:, :LANES]
-            slot[half_at:half_at + rows // 2, :] = jnp.concatenate(
+            hs[k // inner_dp, k % inner_dp, :rows // 2, :] = jnp.concatenate(
                 [mine[:rows // 2, LANES:LANES + half], mine[rows // 2:, LANES:LANES + half]], axis=1)
-            slot[sums_at:, :] = extra
+            slot[half_at:, :] = extra
 
         def p_copy(o, bufs):
             src, dst, _, _, ss, rs, _, _ = bufs
@@ -407,6 +408,18 @@
         first = (gs1, pv1, gm1, gr1, ps1, pr1, g1s, g1r)
         second = (gs2, pv2, gm2, gr2, ps2, pr2, g2s, g2r)
         order = [ranked(1, n) for n in reversed(range(outer_dp - 1))] + [0]
+
+        def h_copy(o):
+            to = lax.rem(far + o, outer_dp)
+            return pltpu.make_async_remote_copy(
+                src_ref=hs.at[to], dst_ref=hr.at[o - 1], send_sem=hss, recv_sem=hrs,
+                device_id=(line(o), mp), device_id_type=MESH)
+
+        h_pair = pltpu.make_async_remote_copy(
+            src_ref=ht.at[other], dst_ref=hv, send_sem=hps, recv_sem=hpr,
+            device_id=(partner, mp), device_id_type=MESH)
+        for o in order[:-1]:
+            h_copy(o).start()
         for o in order:
             p_copy(o, first).start()
 
@@ -447,16 +460,28 @@
                     mid_buf[o - 1] = pair
                     g_copy(o, bufs).start()
             pairs.append(pair)
+            if bufs is first:
+                arrive(hr, hrs)
+                both = hs[far]
+                for o in range(outer_dp - 1):
+                    both = both + hr[o]
+                ht[...] = both
+                h_pair.start()
         for n, bufs in enumerate((first, second)):
             arrive(bufs[3], bufs[7])
             for o in range(1, outer_dp):
                 pairs[n] = pairs[n] + bufs[3][o - 1]
-        outv[:late_at, :] = pairs[0]
+        h_pair.wait_recv()
+        packed = ht[near] + hv[...]
+        outv[:half_at, :] = pairs[0][:half_at]
+        outv[half_at:sums_at, :] = packed
+        outv[sums_at:late_at, :] = pairs[0][half_at:]
         outv[late_at:total_rows, :] = pairs[1]
-        head = pairs[0][:sums_at]
-        sums = pairs[0][sums_at:]
+        head = pairs[0][:half_at]
+        sums = pairs[0][half_at:]
         bias_grad = sums[:tiles]
         square = jnp.sum(head * head, keepdims=True) + jnp.sum(pairs[1] * pairs[1], keepdims=True)
+        square = square + jnp.sum(packed * packed, keepdims=True)
         bias_square = jnp.sum(bias_grad * bias_grad, keepdims=True)
         lane = lax.broadcasted_iota(jnp.int32, (1, LANES), 1)
         fsend[...] = jnp.where(lane == 0, square + bias_square * (1.0 / ndp), sums[tiles:tiles + 1, :])
@@ -474,6 +499,8 @@
         frecv[me] = fsend[...]
         arrive(wall.at[pl.ds(0, outer_dp - 1)], wss)
         arrive(wall.at[pl.ds(0, outer_dp)], whs)
+        arrive(hs.at[pl.ds(0, outer_dp - 1)], hss)
+        h_pair.wait_send()
         for bufs in (first, second):
             arrive(bufs[0].at[0], bufs[4])
             arrive(bufs[2], bufs[6])
@@ -505,17 +532,24 @@
     dma = pltpu.SemaphoreType.DMA
     vmem = pl.BlockSpec(memory_space=pltpu.VMEM)
     hbm = pl.BlockSpec(memory_space=pl.ANY)
-    _, _, late_at, total_rows = layout(rows)
+    half_at, sums_at, late_at, total_rows = layout(rows)
     inner_dp = 2
     outer_dp = ndp // inner_dp
     exchange = []
-    for n in (late_at, total_rows - late_at):
+    for n in (half_at + 8, total_rows - late_at):
         exchange += [
             pltpu.VMEM((inner_dp, outer_dp, n, LANES), F32),
             pltpu.VMEM((outer_dp, n, LANES), F32),
             pltpu.VMEM((outer_dp - 1, n, LANES), F32),
             pltpu.VMEM((outer_dp - 1, n, LANES), F32),
         ]
+    held = sums_at - half_at
+    exchange += [
+        pltpu.VMEM((outer_dp, inner_dp, held, LANES), F32),
+        pltpu.VMEM((outer_dp - 1, inner_dp, held, LANES), F32),
+        pltpu.VMEM((inner_dp, held, LANES), F32),
+        pltpu.VMEM((held, LANES), F32),
+    ]
     exchange_sems = [dma(()), dma((outer_dp,)), dma(()), dma(())]
     summed = pl.pallas_call(
         functools.partial(kernel, ndp, nmp),
@@ -553,7 +587,7 @@
             pltpu.VMEM((ntot, 1, LANES), F32),
             dma((groups,)), dma((groups,)), dma((2,)), dma(()),
             dma(()), dma((outer_dp,)), dma(()), dma(()), dma(()), dma((groups,)),
-        ] + exchange_sems * 2 + [dma(()), dma(())],
+        ] + exchange_sems * 2 + [dma(())] * 6,
         compiler_params=pltpu.CompilerParams(
             collective_id=0, has_side_effects=True, vmem_limit_bytes=60 * 1024 * 1024
         ),

time: 41.2 us -> 40.8 us (level)
    pallas_call x1, Pallas kernels: 39.7 us -> 39.2 us  [body(): pl.pallas_call(functools.partial(kernel, ndp, nmp), out_shape=pltpu.VMEM(...]
where the time goes in v5:
time: 40.8 us; the launch traced here: 40.6 us
  Pallas kernels  40 us (98%)
  between operations  0.64 us (2%)
    pallas_call x1, Pallas kernels, body(): pl.pallas_call(functools.partial(kernel, ndp, nmp), out_shape=pltpu.VMEM(...  39.2 us

profile of v5, /device:TPU:0, one launch (start us, length us, event | category | flops | bytes accessed | tf_op | source)
XLA Modules:
  0.0 40.6 jit_solution(4134641396277461551)
XLA Ops:
  0.6 39.2 %shard_map.84.sum_ref = f32[136,128]{1,0:T(8,128)S(1)} custom-call(bf16[16384,384]{1,0:T(8,128)(2,1)} %bitcast.4, bf16[48,320]{1,0:T(8,128)(2,1)} %w_hbm.1, f32[320]{0:T(512)} %b_hbm.1, bf16[64,320,256]{2,1,0:T(8,128)(2,1)} %bitcast.5, s32[64,4,256]{2,1,0:T(4,128)} %m_hbm.1), custom_call_target="tpu_custom_call" | custom-call | tf_op jit(solution)/shard_map/pallas_call | solution.py:554
  39.9 0.8 %shard_map.85 = (f32[1,1]{1,0:T(1,128)}, f32[1,1]{1,0:T(1,128)}, f32[48,320]{1,0:T(8,128)}, f32[320]{0:T(512)}) custom-call(f32[136,128]{1,0:T(8,128)S(1)} %shard_map.84.sum_ref), custom_call_target="tpu_custom_call" | custom-call | tf_op jit(solution)/shard_map/pallas_call | solution.py:601

commit v6 on v5

--- a/solution.py
+++ b/solution.py
@@ -365,13 +365,13 @@
 
         lax.fori_loop(0, groups, outer, 0)
         project(0, 0)
-        for q in mxus:
-            pltpu.matmul_pop(proj[q][0])
         for g in range(PAIR):
             push_gradient(steps - 1, g)
             gradient(sb, g)
         acc1[:rest, :TILE] = pltpu.matmul_pop(grad_acc[0])
         acc1[:rest, TILE:] = pltpu.matmul_pop(grad_acc[1])[:, :width - TILE]
+        for q in mxus:
+            pltpu.matmul_pop(proj[q][0])
 
         half_at, sums_at, late_at, total_rows = layout(rows)
         tiles = featp // LANES
@@ -441,14 +441,14 @@
         lax.fori_loop(0, images // SWEEP, sweep, 0)
         acc2[:, :TILE] = pltpu.matmul_pop(late_acc[0])
         acc2[:, TILE:] = pltpu.matmul_pop(late_acc[1])[:, :width - TILE]
-        for q in mxus:
-            pltpu.matmul_acc_lhs(late_acc[q], jnp.zeros((early, TILE), BF16), load_staged_rhs=0)
-            pltpu.matmul_pop(late_acc[q])
         full = jnp.transpose(acc2[...])
         for k in range(ndp):
             gs2[k % inner_dp, k // inner_dp, :rows, :] = full[k * rows:(k + 1) * rows]
         for o in order:
             p_copy(o, second).start()
+        for q in mxus:
+            pltpu.matmul_acc_lhs(late_acc[q], jnp.zeros((early, TILE), BF16), load_staged_rhs=0)
+            pltpu.matmul_pop(late_acc[q])
 
         pairs = []
         for bufs in (first, second):

time: 40.8 us -> 40.8 us (level)
  no operation moved by 1% of the time
where the time goes in v6:
time: 40.8 us; the launch traced here: 40.6 us
  Pallas kernels  40 us (98%)
  between operations  0.64 us (2%)
    pallas_call x1, Pallas kernels, body(): pl.pallas_call(functools.partial(kernel, ndp, nmp), out_shape=pltpu.VMEM(...  39.2 us

profile of v6, /device:TPU:0, one launch (start us, length us, event | category | flops | bytes accessed | tf_op | source)
XLA Modules:
  0.0 40.6 jit_solution(4951405346440223182)
XLA Ops:
  0.6 39.2 %shard_map.84.sum_ref = f32[136,128]{1,0:T(8,128)S(1)} custom-call(bf16[16384,384]{1,0:T(8,128)(2,1)} %bitcast.4, bf16[48,320]{1,0:T(8,128)(2,1)} %w_hbm.1, f32[320]{0:T(512)} %b_hbm.1, bf16[64,320,256]{2,1,0:T(8,128)(2,1)} %bitcast.5, s32[64,4,256]{2,1,0:T(4,128)} %m_hbm.1), custom_call_target="tpu_custom_call" | custom-call | tf_op jit(solution)/shard_map/pallas_call | solution.py:554
  39.9 0.8 %shard_map.85 = (f32[1,1]{1,0:T(1,128)}, f32[1,1]{1,0:T(1,128)}, f32[48,320]{1,0:T(8,128)}, f32[320]{0:T(512)}) custom-call(f32[136,128]{1,0:T(8,128)S(1)} %shard_map.84.sum_ref), custom_call_target="tpu_custom_call" | custom-call | tf_op jit(solution)/shard_map/pallas_call | solution.py:601
